TPU v7x, 32 devices: a whole 2x2x4 slice. The times are simulated.
32 devices in a mesh: train: 4 (over y, x), induce: 8 (over z, core).
Axes of the slice: x: 2, y: 2, z: 4, core: 2. Of those that a mesh axis runs over, the one named last changes fastest.
Arguments:
- train_coords: float32 [256, 192], P('train'), may hold values from -0.3 to 4.8, as said below
- induce_coords: float32 [1024, 192], P('induce'), may hold values from -0.3 to 4.8, as said below
- train_forces: float32 [256, 192], P('train'), may hold values from -18 to 18
- atom_pairs: int32 [2, 2016], replicated, may hold values from 0 to 63, as said below
- length_scale: float32 [1], replicated, may hold values from 1.5 to 3
Outputs:
- coefficients: float32 [1024, 192], P('induce')
- residual: float32 [1024, 192], P('induce')
- desc_coeffs: float32 [1024, 2016], P('induce')
Inputs may be any that keep to these rules, and one draw needn't show every extreme that they name: `atom_pairs`: every unordered pair of two different atoms of the 64 stands in exactly one column, in either order. `train_coords`: atom a lies within 0.3 of 1.5 * (a % 4, a // 4 % 4, a // 16) in each component. `induce_coords`: atom a lies within 0.3 of 1.5 * (a % 4, a // 4 % 4, a // 16) in each component.
All inputs are finite; a program needn't handle non-finite values.
Results may differ from a plain program's by a relative error of at most 0.0085.
Values sent between devices are 32-bit elements; how exact they have to be, the bound alone decides.
No kernel may reach another device: no remote copies, remote signals or barrier semaphores. Data moves between devices by JAX's collectives and lax.ppermute only.
A program may use at most 64 MiB of HBM per device.

v0:
```python
import math

import jax
import jax.numpy as jnp
from jax import lax
from jax.sharding import PartitionSpec as P

root_five = math.sqrt(5.0)


def make_incidence(atom_pairs, atom_count):
    atom_ids = jnp.arange(atom_count, dtype=jnp.int32)
    head_hit = (atom_pairs[0][:, None] == atom_ids[None, :]).astype(jnp.float32)
    tail_hit = (atom_pairs[1][:, None] == atom_ids[None, :]).astype(jnp.float32)
    return head_hit - tail_hit


def lattice_coords(atom_count):
    atom_ids = jnp.arange(atom_count, dtype=jnp.int32)
    lattice = jnp.stack([atom_ids % 4, atom_ids // 4 % 4, atom_ids // 16]).astype(jnp.float32)
    return (1.5 * lattice).reshape(1, 3 * atom_count)


def describe(coords, incidence):
    atom_count = incidence.shape[1]
    spatial = coords.reshape(coords.shape[0], 3, atom_count)
    offsets = jnp.einsum("bca,pa->bcp", spatial, incidence, precision=lax.Precision.HIGHEST)
    length = jnp.sqrt(jnp.sum(offsets * offsets, axis=1))
    return (1.0 / length, offsets / (length**3)[:, None, :])


def centered(coords, incidence):
    values, gradients = describe(coords, incidence)
    lattice_values = describe(lattice_coords(incidence.shape[1]), incidence)[0]
    return ((values - lattice_values).astype(jnp.bfloat16), gradients)


def to_desc(gradients, vectors, incidence):
    atom_count = incidence.shape[1]
    shifted = jnp.einsum(
        "bca,pa->bcp",
        vectors.reshape(vectors.shape[0], 3, atom_count),
        incidence,
        precision=lax.Precision.HIGHEST,
    )
    return -jnp.sum(gradients * shifted, axis=1)


def to_forces(gradients, values, incidence):
    weighted = gradients * values[:, None, :]
    summed = jnp.einsum("bcp,pa->bca", weighted, incidence, precision=lax.Precision.HIGHEST)
    return -summed.reshape(values.shape[0], -1)


def matern(row_desc, col_desc, length):
    inner_prod = jnp.dot(row_desc, col_desc.T, preferred_element_type=jnp.float32)
    row_sq = jnp.sum(jnp.square(row_desc.astype(jnp.float32)), axis=1)
    col_sq = jnp.sum(jnp.square(col_desc.astype(jnp.float32)), axis=1)
    radius = jnp.sqrt(row_sq[:, None] + col_sq[None, :] - 2.0 * inner_prod) / length
    falloff = jnp.exp(-root_five * radius)
    diag_part = 5.0 / (3.0 * length**2) * (1.0 + root_five * radius) * falloff
    outer_part = 25.0 / (3.0 * length**4) * falloff
    return (diag_part, outer_part)


def apply_forward(train_desc, induce_desc, diag_part, outer_part, induce_vals):
    self_dot = jnp.sum(induce_desc.astype(jnp.float32) * induce_vals.astype(jnp.float32), axis=1)
    projected = (
        jnp.dot(train_desc, induce_vals.T, preferred_element_type=jnp.float32) - self_dot[None, :]
    )
    product = outer_part * projected
    result = jnp.dot(
        diag_part.astype(jnp.bfloat16), induce_vals, preferred_element_type=jnp.float32
    )
    result = result + jnp.dot(
        product.astype(jnp.bfloat16), induce_desc, preferred_element_type=jnp.float32
    )
    return result - train_desc.astype(jnp.float32) * jnp.sum(product, axis=1)[:, None]


def apply_adjoint(train_desc, induce_desc, diag_part, outer_part, train_vals):
    self_dot = jnp.sum(train_desc.astype(jnp.float32) * train_vals.astype(jnp.float32), axis=1)
    projected = self_dot[:, None] - jnp.dot(
        train_vals, induce_desc.T, preferred_element_type=jnp.float32
    )
    product = outer_part * projected
    result = jnp.dot(
        diag_part.astype(jnp.bfloat16).T, train_vals, preferred_element_type=jnp.float32
    )
    result = result - jnp.dot(
        product.astype(jnp.bfloat16).T, train_desc, preferred_element_type=jnp.float32
    )
    return result + induce_desc.astype(jnp.float32) * jnp.sum(product, axis=0)[:, None]


def per_device(train_coords, induce_coords, train_forces, atom_pairs, length_scale):
    atom_count = train_coords.shape[1] // 3
    incidence = make_incidence(atom_pairs, atom_count)
    train_desc, train_grad = centered(train_coords, incidence)
    induce_desc, induce_grad = centered(induce_coords, incidence)
    diag_part, outer_part = matern(train_desc, induce_desc, length_scale[0])

    def forward(vectors):
        vectors = lax.all_gather(vectors, "train", axis=0, tiled=True)
        induce_vals = to_desc(induce_grad, vectors, incidence).astype(jnp.bfloat16)
        partial_forces = to_forces(
            train_grad,
            apply_forward(train_desc, induce_desc, diag_part, outer_part, induce_vals),
            incidence,
        )
        return lax.psum(partial_forces, "induce")

    def adjoint(forces_like):
        train_vals = to_desc(train_grad, forces_like, incidence).astype(jnp.bfloat16)
        partial_coeffs = to_forces(
            induce_grad,
            apply_adjoint(train_desc, induce_desc, diag_part, outer_part, train_vals),
            incidence,
        )
        return lax.psum_scatter(partial_coeffs, "train", scatter_dimension=0, tiled=True)

    start = adjoint(train_forces)
    probed = forward(start)
    probed_local = jnp.sum(probed * probed)
    cross_local = jnp.sum(train_forces * probed)
    probed_sq = lax.psum(probed_local, "train")
    cross_sq = lax.psum(cross_local, "train")
    quotient = probed_sq / cross_sq
    center = 0.775 * quotient
    spread = 0.725 * quotient
    momentum = spread / center
    direction = start / center
    coefficients = direction
    residual = start - adjoint(probed) / center
    momentum_next = 1.0 / (2.0 * center / spread - momentum)
    direction = momentum_next * momentum * direction + 2.0 * momentum_next / spread * residual
    coefficients = coefficients + direction
    residual = residual - adjoint(forward(direction))
    coefficients, residual = (
        lax.all_gather(coefficients, "train", axis=0, tiled=True),
        lax.all_gather(residual, "train", axis=0, tiled=True),
    )
    desc_coeffs = to_desc(induce_grad, coefficients, incidence)
    return (coefficients, residual, desc_coeffs)


def solution(mesh):
    in_specs = (P("train", None), P("induce", None), P("train", None), P(), P())
    out_specs = (P("induce", None), P("induce", None), P("induce", None))
    return jax.shard_map(
        per_device, mesh=mesh, in_specs=in_specs, out_specs=out_specs, check_vma=False
    )
```

profile of v0, /device:TPU:0, one launch (start us, length us, event | category | flops | bytes accessed | tf_op | source)
XLA Modules:
  0.0 235.9 jit_solution(11568177319664420499)
XLA Ops:
  12.8 4.5 %fusion = (f32[128,2016]{0,1:T(8,128)S(1)}, f32[2016,128,3]{1,0,2:T(8,128)}) fusion(f32[128,3,64]{0,2,1:T(8,128)S(1)} %bitcast.109, s32[2016]{0:T(1024)S(1)} %bitcast.136, s32[2016]{0:T(1024)S(1)} %bitcast.122), kind=kOutput, calls=%fused_computation.2 | convolution fusion | flops 596477952 | bytes 4243200 | tf_op jit(solution)/shard_map/bca,pa->bcp/dot_general | solution.py:27
  22.3 2.3 fusion.29
  25.4 27.0 %reduce-scatter.10.cloned.1.call-done = f32[32,192]{1,0:T(8,128)} async-done(((f32[128,192]{1,0:T(8,128)}), f32[32,192]{1,0:T(8,128)}) %reduce-scatter.10.cloned.1.call-update) | async-done | bytes 24592 | tf_op jit(solution)/shard_map/reduce_scatter | solution.py:120
  52.4 8.6 %all_gather.12 = f32[128,192]{1,0:T(8,128)S(1)} all-gather(f32[32,192]{1,0:T(8,128)} %reduce-scatter.10.cloned.1.call-done), channel_id=1, replica_groups=mesh['train'=4,'induce'=8] {'train'}, dimensions={0}, use_global_device_ids=true | all-gather | bytes 122880 | tf_op jit(solution)/shard_map/all_gather | solution.py:104
  61.1 5.3 %multiply_reduce_fusion.2 = f32[128,2016]{0,1:T(8,128)S(1)} fusion(f32[128,3,64]{0,2,1:T(8,128)S(1)} %bitcast.116, s32[2016]{0:T(1024)S(1)} %bitcast.139, s32[2016]{0:T(1024)S(1)} %bitcast.125, f32[128,2016]{0,1:T(8,128)S(1)} %get-tuple-element.20, f32[2016,128,3]{1,0,2:T(8,128)} %get-tuple-element.26), kind=kOutput, calls=%fused_computation.9 | convolution fusion | flops 597252096 | bytes 5275392 | tf_op jit(solution)/shard_map/bca,pa->bcp/dot_general | solution.py:40
  67.9 2.2 fusion.23
  71.7 28.0 %psum.28 = f32[64,192]{0,1:T(8,128)} all-reduce(f32[64,192]{0,1:T(8,128)} %bitcast.113), channel_id=1, replica_groups=mesh['train'=4,'induce'=8] {'induce'}, use_global_device_ids=true, to_apply=%region_12.13 | all-reduce | flops 12288 | bytes 98304 | tf_op jit(solution)/shard_map/psum | solution.py:111
  99.7 2.8 %fusion.21 = f32[64,2016]{1,0:T(8,128)S(1)} fusion(f32[64,3,64]{0,2,1:T(8,128)} %bitcast.112, s32[2016]{0:T(1024)S(1)} %bitcast.141, s32[2016]{0:T(1024)S(1)} %bitcast.127, f32[64,3,2016]{2,0,1:T(8,128)S(1)} %copy-done.5, f32[64,2016]{1,0:T(8,128)} %copy-done.6), kind=kOutput, calls=%fused_computation.44 | convolution fusion | flops 298948608 | bytes 2645760 | tf_op jit(solution)/shard_map/bca,pa->bcp/dot_general | solution.py:40
  104.4 2.9 %fusion.32 = f32[128,3,64]{0,2,1:T(8,128)} fusion(f32[128,2016]{0,1:T(8,128)S(1)} %fusion.9, s32[2016]{0:T(1024)S(1)} %bitcast.142, s32[2016]{0:T(1024)S(1)} %bitcast.128, f32[2016,128,3]{1,0,2:T(8,128)S(1)} %copy-done.2, f32[128,2016]{0,1:T(8,128)S(1)} %get-tuple-element.20), kind=kOutput, calls=%fused_computation.55 | convolution fusion | flops 596760576 | bytes 5275392 | tf_op jit(solution)/shard_map/bcp,pa->bca/dot_general | solution.py:51
  109.0 1.6 multiply_reduce_fusion.4
  110.7 9.5 %all-reduce = (f32[]{:T(128)}, f32[]{:T(128)}) all-reduce(f32[]{:T(128)} %get-tuple-element.12, f32[]{:T(128)} %get-tuple-element.11), channel_id=1, replica_groups=mesh['train'=4,'induce'=8] {'train'}, use_global_device_ids=true, to_apply=%region_14.15 | all-reduce | flops 2 | bytes 16 | tf_op jit(solution)/shard_map/psum | solution.py:126
  121.7 8.8 %reduce-scatter.12.cloned.1.call-done = f32[32,192]{1,0:T(8,128)} async-done(((f32[128,192]{1,0:T(8,128)}), f32[32,192]{1,0:T(8,128)}) %reduce-scatter.12.cloned.1.call-update) | async-done | bytes 24592 | tf_op jit(solution)/shard_map/reduce_scatter | solution.py:120
  131.9 9.3 %all_gather.14 = f32[128,192]{1,0:T(8,128)} all-gather(f32[32,192]{1,0:T(8,128)S(1)} %get-tuple-element.16), channel_id=1, replica_groups=mesh['train'=4,'induce'=8] {'train'}, dimensions={0}, use_global_device_ids=true | all-gather | bytes 122880 | tf_op jit(solution)/shard_map/all_gather | solution.py:104
  141.2 1.6 copy.45
  142.8 5.3 %multiply_reduce_fusion.1 = f32[128,2016]{0,1:T(8,128)S(1)} fusion(f32[128,3,64]{0,2,1:T(8,128)} %bitcast.118, s32[2016]{0:T(1024)S(1)} %bitcast.143, s32[2016]{0:T(1024)S(1)} %bitcast.129, f32[128,2016]{0,1:T(8,128)S(1)} %get-tuple-element.20, f32[2016,128,3]{1,0,2:T(8,128)} %get-tuple-element.26), kind=kOutput, calls=%fused_computation.6 | convolution fusion | flops 597252096 | bytes 5275392 | tf_op jit(solution)/shard_map/bca,pa->bcp/dot_general | solution.py:40
  149.5 2.2 fusion.26
  151.6 27.5 %psum.31 = f32[64,3,64]{2,0,1:T(8,128)S(1)} all-reduce(f32[64,3,64]{2,0,1:T(8,128)} %fusion.26), channel_id=1, replica_groups=mesh['train'=4,'induce'=8] {'induce'}, use_global_device_ids=true, to_apply=%region_24.25 | all-reduce | flops 12288 | bytes 98304 | tf_op jit(solution)/shard_map/psum | solution.py:111
  179.1 3.1 %fusion.22 = f32[64,2016]{1,0:T(8,128)S(1)} fusion(f32[64,3,64]{2,0,1:T(8,128)S(1)} %psum.31, s32[2016]{0:T(1024)S(1)} %bitcast.145, s32[2016]{0:T(1024)S(1)} %bitcast.131, f32[64,3,2016]{2,0,1:T(8,128)} %copy-done.4, f32[64,2016]{1,0:T(8,128)} %copy-done.6), kind=kOutput, calls=%fused_computation.45 | convolution fusion | flops 298948608 | bytes 2645760 | tf_op jit(solution)/shard_map/bca,pa->bcp/dot_general | solution.py:40
  182.8 8.5 %all_gather.13 = f32[128,192]{1,0:T(8,128)} all-gather(f32[32,192]{1,0:T(8,128)S(1)} %copy-done.11), channel_id=1, replica_groups=mesh['train'=4,'induce'=8] {'train'}, dimensions={0}, use_global_device_ids=true | all-gather | bytes 122880 | tf_op jit(solution)/shard_map/all_gather | solution.py:140
  191.2 1.6 copy.48
  194.8 2.3 fusion.35
  197.8 5.3 %multiply_reduce_fusion = f32[128,2016]{0,1:T(8,128)S(1)} fusion(f32[128,3,64]{0,2,1:T(8,128)S(1)} %bitcast.114, s32[2016]{0:T(1024)S(1)} %bitcast.147, s32[2016]{0:T(1024)S(1)} %bitcast.133, f32[128,2016]{0,1:T(8,128)S(1)} %get-tuple-element.20, f32[2016,128,3]{1,0,2:T(8,128)} %get-tuple-element.26), kind=kOutput, calls=%fused_computation.3 | convolution fusion | flops 597252096 | bytes 5275392 | tf_op jit(solution)/shard_map/bca,pa->bcp/dot_general | solution.py:40
  204.2 15.2 %reduce-scatter.14.cloned.1.call-done = f32[32,192]{1,0:T(8,128)} async-done(((f32[128,192]{1,0:T(8,128)}), f32[32,192]{1,0:T(8,128)}) %reduce-scatter.14.cloned.1.call-update) | async-done | bytes 24592 | tf_op jit(solution)/shard_map/reduce_scatter | solution.py:120
  220.1 8.5 %all_gather.15 = f32[128,192]{1,0:T(8,128)S(1)} all-gather(f32[32,192]{1,0:T(8,128)S(1)} %fusion.115), channel_id=1, replica_groups=mesh['train'=4,'induce'=8] {'train'}, dimensions={0}, use_global_device_ids=true | all-gather | bytes 122880 | tf_op jit(solution)/shard_map/all_gather | solution.py:141
  (75 shorter events, 25.8 us)
Async XLA Ops:
  7.2 5.7 %copy-start = (f32[128,192]{0,1:T(8,128)S(1)}, f32[128,192]{0,1:T(8,128)}, u32[]{:S(2)}) copy-start(f32[128,192]{0,1:T(8,128)} %param.6) | copy-start | bytes 294916
  7.2 45.2 %reduce-scatter.10.cloned.1.call-start = ((), (), s32[]{:S(2)}) async-start(), calls=%async_computation.3 | async-start | bytes 163840 | tf_op jit(solution)/shard_map/reduce_scatter | solution.py:120
  10.2 7.2 %copy-start.9 = (f32[64,192]{0,1:T(8,128)}, f32[64,192]{0,1:T(8,128)S(1)}, u32[]{:S(2)}) copy-start(f32[64,192]{0,1:T(8,128)S(1)} %copy.35) | copy-start | bytes 147460
  12.6 6.3 %copy-start.4 = (f32[64,3,2016]{2,0,1:T(8,128)}, f32[64,3,2016]{2,0,1:T(8,128)S(1)}, u32[]{:S(2)}) copy-start(f32[64,3,2016]{2,0,1:T(8,128)S(1)} %get-tuple-element.24) | copy-start | bytes 4644868
  12.8 6.2 %copy-start.6 = (f32[64,2016]{1,0:T(8,128)}, f32[64,2016]{1,0:T(8,128)S(1)}, u32[]{:S(2)}) copy-start(f32[64,2016]{1,0:T(8,128)S(1)} %multiply_multiply_fusion.1) | copy-start | bytes 1548292
  20.5 1.9 copy-start.1
  25.4 105.1 %reduce-scatter.12.cloned.1.call-start = ((), (), s32[]{:S(2)}) async-start(), calls=%async_computation.4 | async-start | bytes 163840 | tf_op jit(solution)/shard_map/reduce_scatter | solution.py:120
  66.4 1.4 copy-start.5
  66.4 1.5 copy-start.7
  102.5 1.9 copy-start.2
  109.0 110.4 %reduce-scatter.14.cloned.1.call-start = ((), (), s32[]{:S(2)}) async-start(), calls=%async_computation.5 | async-start | bytes 163840 | tf_op jit(solution)/shard_map/reduce_scatter | solution.py:120
  148.1 1.3 copy-start.8
  179.1 3.7 %copy-start.11 = (f32[32,192]{1,0:T(8,128)S(1)}, f32[32,192]{1,0:T(8,128)}, u32[]{:S(2)}) copy-start(f32[32,192]{1,0:T(8,128)} %get-tuple-element.15) | copy-start | bytes 73732
  192.9 1.9 copy-start.3
  194.7 3.0 %copy-start.13 = (f32[128,192]{0,1:T(8,128)S(1)}, f32[128,192]{0,1:T(8,128)}, u32[]{:S(2)}) copy-start(f32[128,192]{0,1:T(8,128)} %copy.48) | copy-start | bytes 294916
  197.8 21.5 %copy-start.10 = (f32[32,192]{1,0:T(8,128)S(1)}, f32[32,192]{1,0:T(8,128)}, u32[]{:S(2)}) copy-start(f32[32,192]{1,0:T(8,128)} %reduce-scatter.10.cloned.1.call-done) | copy-start | bytes 73732
  197.8 21.5 %copy-start.12 = (f32[32,192]{1,0:T(8,128)S(1)}, f32[32,192]{1,0:T(8,128)}, u32[]{:S(2)}) copy-start(f32[32,192]{1,0:T(8,128)} %reduce-scatter.12.cloned.1.call-done) | copy-start | bytes 73732
Sparse Core Ops, SparseCore 0:
  25.5 26.8 reduce-scatter.9
  109.1 21.3 reduce-scatter.11
  197.9 21.3 reduce-scatter.13
where the time goes:
time: 237 us; the launch traced here: 236 us
  blocking collectives  99.8 us (42%)
  waiting for transfers between devices  51 us (22%)
  matrix products  46.9 us (20%)
  between operations  16.3 us (7%)
  local copies, waits for them, and re-layouts  15 us (6%)
  other arithmetic  6.73 us (3%)
    psum x2, blocking collectives, forward(): return lax.psum(partial_forces, 'induce')  55.5 us
    reduce_scatter x3, waiting for transfers between devices, adjoint(): lax.psum_scatter(partial_coeffs, 'train', scatter_dimension=0, tiled=True)  51 us
    dot_general x6, matrix products, to_desc(): jnp.einsum('bca,pa->bcp', vectors.reshape(vectors.shape[0], 3, atom_count...  23.4 us
    all_gather x2, blocking collectives, forward(): vectors = lax.all_gather(vectors, 'train', axis=0, tiled=True)  17.8 us
    dot_general x5, matrix products, to_forces(): jnp.einsum('bcp,pa->bca', weighted, incidence, precision=lax.Precision.HI...  11.7 us
    unnamed x35, local copies, waits for them, and re-layouts  10.8 us
    psum x1, blocking collectives, per_device(): probed_sq = lax.psum(probed_local, 'train')  9.53 us
    all_gather x1, blocking collectives, per_device(): lax.all_gather(residual, 'train', axis=0, tiled=True)  8.46 us
  transfers between devices with their start and end apart: 3, of which 3 were waited for; matrix products, arithmetic and copies ran while one was open for 3% of the time, Pallas kernels for 0%

commit v1 on v0

v1 whole, which is shorter than its diff:
```python
import functools
import math

import jax
import jax.numpy as jnp
from jax import lax
from jax.experimental import pallas as pl
from jax.experimental.pallas import tpu as pltpu
from jax.sharding import PartitionSpec as P

root_five = math.sqrt(5.0)
f32 = jnp.float32
bf16 = jnp.bfloat16
BLOCK = 128
CHUNK = 512
GATHER = 4
VMEM_LIMIT = 60 * 1024 * 1024


def dot(lhs, rhs, rhs_contract=0):
    return lax.dot_general(
        lhs, rhs, (((1,), (rhs_contract,)), ((), ())), preferred_element_type=f32
    )


def split_three(x):
    high = x.astype(bf16)
    rest = x - high.astype(f32)
    mid = rest.astype(bf16)
    low = (rest - mid.astype(f32)).astype(bf16)
    return jnp.concatenate([high, mid, low], axis=1)


def put_split(split_ref, start, values, atoms):
    rows = values.shape[0]
    for comp in range(3):
        part = values[:, comp * atoms : (comp + 1) * atoms]
        split_ref[comp, pl.ds(start, rows), :] = split_three(part)


def build_incidence(pairs_ref, inc_ref, inc_t_ref):
    atoms = inc_t_ref.shape[1]
    count = pairs_ref.shape[1]
    wide = inc_ref.shape[1]
    ids = lax.broadcasted_iota(jnp.int32, (atoms, count), 0)
    signs = (pairs_ref[0:1, :] == ids).astype(f32) - (pairs_ref[1:2, :] == ids).astype(f32)
    if wide > count:
        signs = jnp.concatenate([signs, jnp.zeros((atoms, wide - count), f32)], axis=1)
    for copy in range(3):
        inc_ref[copy * atoms : (copy + 1) * atoms, :] = signs.astype(bf16)
    inc_t_ref[...] = signs.T.astype(bf16)


def lattice_inverse(inc_ref, atoms, count):
    wide = inc_ref.shape[1]
    ids = lax.broadcasted_iota(jnp.int32, (8, atoms), 1)
    total = jnp.zeros((8, wide), f32)
    for steps in (ids % 4, ids // 4 % 4, ids // 16):
        part = dot((1.5 * steps.astype(f32)).astype(bf16), inc_ref[0:atoms, :])
        total = total + part * part
    lanes = lax.broadcasted_iota(jnp.int32, (8, wide), 1)
    padding = (lanes >= count).astype(f32)
    return lax.rsqrt(total + padding)[0:1, :], padding[0:1, :]


def loop(rows, body):
    block = min(rows, BLOCK)
    if rows == block:
        body(0, block)
        return

    def step(index, carry):
        body(pl.multiple_of(index * block, block), block)
        return carry

    lax.fori_loop(0, rows // block, step, 0)


def describe(split_ref, inc_ref, lat_ref, grad_ref, desc_ref, sq_ref):
    rows, wide = desc_ref.shape

    def body(start, block):
        lhs = split_ref[:, pl.ds(start, block), :].reshape(3 * block, -1)
        sq = jnp.zeros((block, 128), f32)
        for at in range(0, wide, CHUNK):
            cols = slice(at, at + CHUNK)
            off = dot(lhs, inc_ref[:, cols])
            off = [off[c * block : (c + 1) * block] for c in range(3)]
            inv = lax.rsqrt(
                off[0] * off[0] + off[1] * off[1] + off[2] * off[2] + lat_ref[1:2, cols]
            )
            desc = (inv - lat_ref[0:1, cols]).astype(bf16)
            desc_ref[pl.ds(start, block), cols] = desc
            cube = -(inv * inv * inv)
            for comp in range(3):
                grad_ref[comp, pl.ds(start, block), cols] = (off[comp] * cube).astype(grad_ref.dtype)
            wide_desc = desc.astype(f32)
            wide_desc = wide_desc * wide_desc
            for lane in range(0, CHUNK, 128):
                sq = sq + wide_desc[:, lane : lane + 128]
        sq_ref[pl.ds(start, block), :] = jnp.broadcast_to(
            jnp.sum(sq, axis=1, keepdims=True), (block, 128)
        )

    loop(rows, body)


def to_desc(split_ref, inc_ref, grad_ref, desc_ref, out_ref, self_ref):
    rows, wide = out_ref.shape

    def body(start, block):
        lhs = split_ref[:, pl.ds(start, block), :].reshape(3 * block, -1)
        total = jnp.zeros((block, 128), f32)
        for at in range(0, wide, CHUNK):
            cols = slice(at, at + CHUNK)
            diff = dot(lhs, inc_ref[:, cols])
            value = jnp.zeros((block, CHUNK), f32)
            for comp in range(3):
                grad = grad_ref[comp, pl.ds(start, block), cols].astype(f32)
                value = value + grad * diff[comp * block : (comp + 1) * block]
            value = value.astype(bf16)
            out_ref[pl.ds(start, block), cols] = value
            product = value.astype(f32) * desc_ref[pl.ds(start, block), cols].astype(f32)
            for lane in range(0, CHUNK, 128):
                total = total + product[:, lane : lane + 128]
        self_ref[pl.ds(start, block), :] = jnp.broadcast_to(
            jnp.sum(total, axis=1, keepdims=True), (block, 128)
        )

    loop(rows, body)


def mix_to_forces(diag_ref, vals_ref, cross_ref, desc_ref, own_ref, sum_ref, grad_ref, inc_t_ref, put):
    rows = own_ref.shape[0]
    wide = own_ref.shape[1]

    def body(start, block):
        diag = diag_ref[pl.ds(start, block), :]
        cross = cross_ref[pl.ds(start, block), :]
        sums = sum_ref[pl.ds(start, block), 0:1]
        forces = None
        for at in range(0, wide, CHUNK):
            cols = slice(at, at + CHUNK)
            value = dot(diag, vals_ref[:, cols]) + dot(cross, desc_ref[:, cols])
            value = value - own_ref[pl.ds(start, block), cols].astype(f32) * sums
            parts = []
            for comp in range(3):
                grad = grad_ref[comp, pl.ds(start, block), cols].astype(f32)
                parts.append((grad * value).astype(bf16))
            part = dot(jnp.concatenate(parts, axis=0), inc_t_ref[cols, :])
            forces = part if forces is None else forces + part
        put(start, block, [forces[c * block : (c + 1) * block] for c in range(3)])

    loop(rows, body)


def lane_sum(x):
    return jnp.broadcast_to(jnp.sum(x, axis=1, keepdims=True), (x.shape[0], 128))


def adjoint(ctx, put):
    to_desc(ctx.vec_t, ctx.inc, ctx.grad_t, ctx.desc_t, ctx.vals_t, ctx.self_t)
    rows = ctx.desc_t.shape[0]
    block = min(rows, 256)
    for at in range(0, rows, block):
        span = slice(at, at + block)
        project = dot(ctx.vals_t[span, :], ctx.desc_i[...], 1) - ctx.self_t[span, 0:1]
        product = (ctx.outer[span, :] * project).T
        ctx.cross_i[:, span] = product.astype(bf16)
        total = lane_sum(product)
        ctx.sum_i[...] = total if at == 0 else ctx.sum_i[...] + total
    mix_to_forces(
        ctx.diag_i, ctx.vals_t, ctx.cross_i, ctx.desc_t, ctx.desc_i, ctx.sum_i, ctx.grad_i, ctx.inc_t, put
    )


def forward(ctx, put):
    to_desc(ctx.vec_i, ctx.inc, ctx.grad_i, ctx.desc_i, ctx.vals_i, ctx.self_i)
    rows = ctx.desc_t.shape[0]
    block = min(rows, 256)
    self_row = ctx.self_i[...].T[0:1, :]
    for at in range(0, rows, block):
        span = slice(at, at + block)
        project = dot(ctx.desc_t[span, :], ctx.vals_i[...], 1) - self_row
        product = ctx.outer[span, :] * project
        ctx.cross_t[span, :] = product.astype(bf16)
        ctx.sum_t[span, :] = lane_sum(product)
    mix_to_forces(
        ctx.diag_t, ctx.vals_i, ctx.cross_t, ctx.desc_i, ctx.desc_t, ctx.sum_t, ctx.grad_t, ctx.inc_t, put
    )


def matern(ctx, length):
    rows = ctx.desc_t.shape[0]
    block = min(rows, 256)
    col_sq = ctx.self_i[...].T[0:1, :]
    for at in range(0, rows, block):
        span = slice(at, at + block)
        inner = dot(ctx.desc_t[span, :], ctx.desc_i[...], 1)
        square = ctx.self_t[span, 0:1] + col_sq - 2.0 * inner
        radius = root_five * (jnp.sqrt(jnp.maximum(square, 0.0)) / length)
        falloff = jnp.exp(-radius)
        diag = 5.0 / (3.0 * length**2) * (1.0 + radius) * falloff
        ctx.diag_t[span, :] = diag.astype(bf16)
        ctx.diag_i[:, span] = diag.T.astype(bf16)
        ctx.outer[span, :] = 25.0 / (3.0 * length**4) * falloff


class Ctx:
    def __init__(self, names, refs):
        for name, ref in zip(names, refs):
            setattr(self, name, ref)


def scratch_of(rows_t, rows_i, wide, atoms, names):
    kinds = dict(
        inc=((3 * atoms, wide), bf16),
        inc_t=((wide, atoms), bf16),
        lat=((8, wide), f32),
        vec_t=((3, rows_t, 3 * atoms), bf16),
        vec_i=((3, rows_i, 3 * atoms), bf16),
        vals_t=((rows_t, wide), bf16),
        vals_i=((rows_i, wide), bf16),
        self_t=((rows_t, 128), f32),
        self_i=((rows_i, 128), f32),
        sum_t=((rows_t, 128), f32),
        sum_i=((rows_i, 128), f32),
        cross_t=((rows_t, rows_i), bf16),
        cross_i=((rows_i, rows_t), bf16),
    )
    return [pltpu.VMEM(*kinds[name]) for name in names]


def first_kernel(n_train, n_induce, atoms, out_names, scratch_names, *refs):
    coords_t = refs[:n_train]
    forces_t = refs[n_train : 2 * n_train]
    coords_i = refs[2 * n_train : 2 * n_train + n_induce]
    pairs, length_ref = refs[2 * n_train + n_induce : 2 * n_train + n_induce + 2]
    rest = refs[2 * n_train + n_induce + 2 :]
    partial, start_out = rest[:2]
    ctx = Ctx(out_names + scratch_names, rest[2:])
    build_incidence(pairs, ctx.inc, ctx.inc_t)
    lattice, padding = lattice_inverse(ctx.inc, atoms, pairs.shape[1])
    ctx.lat[0:1, :] = lattice
    ctx.lat[1:2, :] = padding
    rows = coords_t[0].shape[0]
    for index, ref in enumerate(coords_t):
        put_split(ctx.vec_t, index * rows, ref[...], atoms)
    describe(ctx.vec_t, ctx.inc, ctx.lat, ctx.grad_t, ctx.desc_t, ctx.self_t)
    for index, ref in enumerate(forces_t):
        put_split(ctx.vec_t, index * rows, ref[...], atoms)
    rows = coords_i[0].shape[0]
    for index, ref in enumerate(coords_i):
        put_split(ctx.vec_i, index * rows, ref[...], atoms)
    describe(ctx.vec_i, ctx.inc, ctx.lat, ctx.grad_i, ctx.desc_i, ctx.self_i)
    matern(ctx, length_ref[0])

    def put_start(start, block, parts):
        for comp in range(3):
            start_out[pl.ds(start, block), comp * atoms : (comp + 1) * atoms] = parts[comp]
            ctx.vec_i[comp, pl.ds(start, block), :] = split_three(parts[comp])

    adjoint(ctx, put_start)

    def put_partial(start, block, parts):
        for comp in range(3):
            partial[pl.ds(start, block), comp * atoms : (comp + 1) * atoms] = parts[comp]

    forward(ctx, put_partial)


def second_kernel(n_sum, n_train, atoms, in_names, scratch_names, *refs):
    parts_in = refs[:n_sum]
    forces_t = refs[n_sum : n_sum + n_train]
    rest = refs[n_sum + n_train :]
    pairs, start_in = rest[:2]
    n_in = len(in_names)
    ctx = Ctx(in_names, rest[2 : 2 + n_in])
    partial, coeffs_out, resid_out = rest[2 + n_in : 5 + n_in]
    for name, ref in zip(scratch_names, rest[5 + n_in :]):
        setattr(ctx, name, ref)
    build_incidence(pairs, ctx.inc, ctx.inc_t)
    rows = forces_t[0].shape[0]
    probed_sq = jnp.zeros((1, 1), f32)
    cross_sq = jnp.zeros((1, 1), f32)
    for index in range(n_train):
        span = slice(index * rows, (index + 1) * rows)
        probed = parts_in[0][span, :]
        for ref in parts_in[1:]:
            probed = probed + ref[span, :]
        put_split(ctx.vec_t, index * rows, probed, atoms)
        probed_sq = probed_sq + jnp.sum(probed * probed, keepdims=True)
        cross_sq = cross_sq + jnp.sum(forces_t[index][...] * probed, keepdims=True)
    quotient = probed_sq / cross_sq
    center = 0.775 * quotient
    spread = 0.725 * quotient
    momentum = spread / center
    momentum_next = 1.0 / (2.0 * center / spread - momentum)

    def put_resid(start, block, parts):
        for comp in range(3):
            cols = slice(comp * atoms, (comp + 1) * atoms)
            first = start_in[pl.ds(start, block), cols]
            resid = first - parts[comp] / center
            direction = first / center
            coeffs = direction
            direction = momentum_next * momentum * direction + 2.0 * momentum_next / spread * resid
            resid_out[pl.ds(start, block), cols] = resid
            coeffs_out[pl.ds(start, block), cols] = coeffs + direction
            ctx.vec_i[comp, pl.ds(start, block), :] = split_three(direction)

    adjoint(ctx, put_resid)

    def put_partial(start, block, parts):
        for comp in range(3):
            partial[pl.ds(start, block), comp * atoms : (comp + 1) * atoms] = parts[comp]

    forward(ctx, put_partial)


def desc_kernel(atoms, coeffs, pairs, grad_i, coeffs_out, out, inc, inc_t, vec):
    build_incidence(pairs, inc, inc_t)
    put_split(vec, 0, coeffs[...], atoms)
    coeffs_out[...] = coeffs[...]
    count = out.shape[1]

    def body(start, block):
        lhs = vec[:, pl.ds(start, block), :].reshape(3 * block, -1)
        for at in range(0, inc.shape[1], CHUNK):
            end = min(at + CHUNK, count)
            diff = dot(lhs, inc[:, at : at + CHUNK])
            value = jnp.zeros((block, CHUNK), f32)
            for comp in range(3):
                grad = grad_i[comp, pl.ds(start, block), at : at + CHUNK].astype(f32)
                value = value + grad * diff[comp * block : (comp + 1) * block]
            out[pl.ds(start, block), at:end] = value[:, : end - at]

    loop(out.shape[0], body)


def third_kernel(n_sum, atoms, in_names, scratch_names, *refs):
    parts_in = refs[:n_sum]
    pairs, resid_in = refs[n_sum : n_sum + 2]
    n_in = len(in_names)
    rest = refs[n_sum + 2 :]
    ctx = Ctx(in_names, rest[:n_in])
    resid_out = rest[n_in]
    for name, ref in zip(scratch_names, rest[n_in + 1 :]):
        setattr(ctx, name, ref)
    build_incidence(pairs, ctx.inc, ctx.inc_t)
    total = parts_in[0][...]
    for ref in parts_in[1:]:
        total = total + ref[...]
    put_split(ctx.vec_t, 0, total, atoms)

    def put_resid(start, block, parts):
        for comp in range(3):
            cols = slice(comp * atoms, (comp + 1) * atoms)
            resid_out[pl.ds(start, block), cols] = resid_in[pl.ds(start, block), cols] - parts[comp]

    adjoint(ctx, put_resid)


def whole(shape):
    return pl.BlockSpec(shape, lambda *_: (0,) * len(shape))


def call(body, ins, specs, outs, scratch):
    return pl.pallas_call(
        body,
        grid=(1,),
        in_specs=specs,
        out_specs=[whole(o.shape) for o in outs],
        out_shape=outs,
        scratch_shapes=scratch,
        compiler_params=pltpu.CompilerParams(vmem_limit_bytes=VMEM_LIMIT),
    )(*ins)


def per_device(n_train, n_induce, train_coords, induce_coords, train_forces, atom_pairs, length_scale):
    atoms = train_coords.shape[1] // 3
    count = atom_pairs.shape[1]
    wide = -(-count // CHUNK) * CHUNK
    gather = math.gcd(GATHER, n_induce // 2)
    rows_t = n_train * train_coords.shape[0]
    own = induce_coords.shape[0]
    rows_i = gather * own

    coords_i = [induce_coords] + [
        lax.ppermute(induce_coords, "induce", [(i, i ^ (2 * step)) for i in range(n_induce)])
        for step in range(1, gather)
    ]
    both = jnp.concatenate([train_coords, train_forces], axis=1)
    both = lax.all_gather(both, "train", axis=0, tiled=True)
    coords_t = [both[:, : 3 * atoms]]
    forces_t = [both[:, 3 * atoms :]]

    grad_dtype = f32 if (rows_t + rows_i) * wide * 12 <= 20 * 1024 * 1024 else bf16
    sds = jax.ShapeDtypeStruct
    kept_names = ["grad_t", "grad_i", "desc_t", "desc_i", "diag_t", "diag_i", "outer"]
    kept = [
        sds((3, rows_t, wide), grad_dtype),
        sds((3, rows_i, wide), grad_dtype),
        sds((rows_t, wide), bf16),
        sds((rows_i, wide), bf16),
        sds((rows_t, rows_i), bf16),
        sds((rows_i, rows_t), bf16),
        sds((rows_t, rows_i), f32),
    ]
    vec_t = sds((rows_t, 3 * atoms), f32)
    vec_i = sds((rows_i, 3 * atoms), f32)
    names = ["inc", "inc_t", "lat", "vec_t", "vec_i", "vals_t", "vals_i", "self_t", "self_i"]
    names += ["sum_t", "sum_i", "cross_t", "cross_i"]
    smem = pl.BlockSpec(memory_space=pltpu.SMEM)
    ins = coords_t + forces_t + coords_i + [atom_pairs]
    partial, start, *state = call(
        functools.partial(first_kernel, len(coords_t), len(coords_i), atoms, kept_names, names),
        ins + [length_scale],
        [whole(x.shape) for x in ins] + [smem],
        [vec_t, vec_i] + kept,
        scratch_of(rows_t, rows_i, wide, atoms, names),
    )

    def reduce_parts(x):
        step = 2 * gather
        while step < n_induce:
            x = x + lax.ppermute(x, "induce", [(i, i ^ step) for i in range(n_induce)])
            step *= 2
        return [x, lax.ppermute(x, "induce", [(i, i ^ 1) for i in range(n_induce)])]

    names = [name for name in names if name != "lat"]
    parts = reduce_parts(partial)
    ins = parts + forces_t + [atom_pairs, start] + state
    partial, coeffs, resid = call(
        functools.partial(second_kernel, len(parts), len(forces_t), atoms, kept_names, names),
        ins,
        [whole(x.shape) for x in ins],
        [vec_t, vec_i, vec_i],
        scratch_of(rows_t, rows_i, wide, atoms, names),
    )
    own_vec = sds((own, 3 * atoms), f32)
    coeffs, desc_coeffs = call(
        functools.partial(desc_kernel, atoms),
        [coeffs, atom_pairs, state[1]],
        [whole(own_vec.shape), whole(atom_pairs.shape), whole((3, own, wide))],
        [own_vec, sds((own, count), f32)],
        scratch_of(rows_t, own, wide, atoms, ["inc", "inc_t", "vec_i"]),
    )
    names = ["inc", "inc_t", "vec_t", "vals_t", "self_t", "sum_i", "cross_i"]
    parts = reduce_parts(partial)
    in_names = ["grad_t", "grad_i", "desc_t", "desc_i", "diag_i", "outer"]
    ins = parts + [atom_pairs, resid] + state[:4] + state[5:]
    specs = [whole(x.shape) for x in parts + [atom_pairs]]
    specs += [whole(own_vec.shape), whole(kept[0].shape), whole((3, own, wide)), whole(kept[2].shape)]
    specs += [whole((own, wide)), whole((own, rows_t)), whole((rows_t, own))]
    (resid,) = call(
        functools.partial(third_kernel, len(parts), atoms, in_names, names),
        ins,
        specs,
        [own_vec],
        scratch_of(rows_t, own, wide, atoms, names),
    )
    return (coeffs, resid, desc_coeffs)


def solution(mesh):
    in_specs = (P("train", None), P("induce", None), P("train", None), P(), P())
    out_specs = (P("induce", None), P("induce", None), P("induce", None))
    body = functools.partial(per_device, mesh.shape["train"], mesh.shape["induce"])
    return jax.shard_map(
        body, mesh=mesh, in_specs=in_specs, out_specs=out_specs, check_vma=False
    )
```

time: 237 us -> 96.1 us (0.41)
  blocking collectives: 99.8 us -> 9.66 us
  Pallas kernels: 0 us -> 66.2 us
  waiting for transfers between devices: 51 us -> 1.74 us
  matrix products: 46.9 us -> 0 us
  between operations: 16.3 us -> 1.38 us
  starting transfers between devices: 0.12 us -> 5.98 us
  other arithmetic: 6.73 us -> 0.95 us
  local copies, waits for them, and re-layouts: 15 us -> 9.81 us
    pallas_call x0 -> x4, Pallas kernels: none -> 66.2 us  [call(): pl.pallas_call(body, grid=(1,), in_specs=specs, out_specs=[whole(o.shape)...]
    psum x3 -> x0, blocking collectives: 65 us -> none  [the longest x2 55.5 us: forward(): return lax.psum(partial_forces, 'induce')]
    reduce_scatter x3 -> x0, waiting for transfers between devices: 51 us -> none  [adjoint(): lax.psum_scatter(partial_coeffs, 'train', scatter_dimension=0, tiled=True)]
    dot_general x30 -> x0, matrix products: 46.9 us -> none  [the longest x6 23.4 us: to_desc(): jnp.einsum('bca,pa->bcp', vectors.reshape(vectors.shape[0], 3, atom_count...]
    all_gather x4 -> x1, blocking collectives: 34.7 us -> 9.66 us  [per_device(): both = lax.all_gather(both, 'train', axis=0, tiled=True)]
    ppermute x0 -> x5, starting transfers between devices: none -> 5.98 us  [the longest x3 5.78 us: per_device(): lax.ppermute(induce_coords, 'induce', [(i, i ^ 2 * step) for i in range(n...]
    reduce_sum x7 -> x0, other arithmetic: 3.34 us -> none  [the longest x1 1.64 us: per_device(): cross_local = jnp.sum(train_forces * probed)]
    unnamed x35 -> x16, local copies, waits for them, and re-layouts: 10.8 us -> 8.91 us
  transfers between devices with their start and end apart: 3 -> 5, of which waited for: 3 -> 1; matrix products, arithmetic and copies ran while one was open for 3% -> 6% of each run, Pallas kernels for 0% -> 4%
where the time goes in v1:
time: 96.1 us; the launch traced here: 95.7 us
  Pallas kernels  66.2 us (69%)
  local copies, waits for them, and re-layouts  9.81 us (10%)
  blocking collectives  9.66 us (10%)
  starting transfers between devices  5.98 us (6%)
  waiting for transfers between devices  1.74 us (2%)
  between operations  1.38 us (1%)
    pallas_call x4, Pallas kernels, call(): pl.pallas_call(body, grid=(1,), in_specs=specs, out_specs=[whole(o.shape)...  66.2 us
    all_gather x1, blocking collectives, per_device(): both = lax.all_gather(both, 'train', axis=0, tiled=True)  9.66 us
    unnamed x16, local copies, waits for them, and re-layouts  8.91 us
    ppermute x3, starting transfers between devices, per_device(): lax.ppermute(induce_coords, 'induce', [(i, i ^ 2 * step) for i in range(n...  5.78 us
  transfers between devices with their start and end apart: 5, of which 1 were waited for; matrix products, arithmetic and copies ran while one was open for 6% of the time, Pallas kernels for 4%

profile of v1, /device:TPU:0, one launch (start us, length us, event | category | flops | bytes accessed | tf_op | source)
XLA Modules:
  0.0 95.7 jit_solution(3459160033880063396)
XLA Ops:
  0.6 1.0 %copy.11.refs_2_ = f32[128,192]{1,0:T(8,128)S(1)} copy(f32[128,192]{0,1:T(8,128)} %param.6) | data formatting | bytes 196608 | tf_op args[1]
  1.6 5.1 %collective-permute-start.2 = (f32[128,192]{1,0:T(8,128)S(1)}, f32[128,192]{1,0:T(8,128)S(1)}, u32[]{:S(2)}, u32[]{:S(2)}) collective-permute-start(f32[128,192]{1,0:T(8,128)S(1)} %copy.11.refs_2_), channel_id=1, source_target_pairs={{0,6},{1,7},{2,4},{3,5},{4,2},{5,3},{6,0},{7,1},{8,14},{9,15},{10,... | collective-permute-start | bytes 294920 | tf_op jit(solution)/shard_map/ppermute | solution.py:390
  6.8 0.0 collective-permute-start.1
  6.8 0.6 collective-permute-start
  7.4 0.9 pad_maximum_fusion
  8.4 9.7 %all_gather.3 = f32[256,384]{1,0:T(8,128)S(1)} all-gather(f32[64,384]{1,0:T(8,128)S(1)} %pad_maximum_fusion), channel_id=1, replica_groups=mesh['train'=4,'induce'=8] {'train'}, dimensions={0}, use_global_device_ids=true | all-gather | bytes 491520 | tf_op jit(solution)/shard_map/all_gather | solution.py:394
  18.0 0.9 fusion
  19.6 0.0 collective-permute-done.2.refs_5_
  19.6 0.0 collective-permute-done.1.refs_4_
  19.7 0.6 copy-done.3
  20.3 0.1 copy-done.4
  20.3 0.0 copy-done.5
  20.3 30.3 %shard_map.76 = (f32[256,192]{1,0:T(8,128)}, f32[512,192]{1,0:T(8,128)}, f32[3,256,2048]{2,1,0:T(8,128)}, f32[3,512,2048]{2,1,0:T(8,128)}, bf16[256,2048]{1,0:T(...) custom-call(f32[256,192]{1,0:T(8,128)} %get-tuple-element.35.refs_0_, ...), custom_call_target="tpu_custom_call" | custom-call | tf_op jit(solution)/shard_map/pallas_call | solution.py:369
  50.6 0.1 collective-permute-start.3
  50.7 1.7 %collective-permute-done.3.refs_1_ = f32[256,192]{1,0:T(8,128)S(1)} collective-permute-done((f32[256,192]{1,0:T(8,128)}, f32[256,192]{1,0:T(8,128)S(1)}, u32[]{:S(2)}, u32[]{:S(2)}) %collective-permute-start.3) | collective-permute-done | bytes 196640 | tf_op jit(solution)/shard_map/ppermute | solution.py:429
  52.4 0.7 copy-done.2
  53.2 23.7 %shard_map.77 = (f32[256,192]{1,0:T(8,128)}, f32[512,192]{1,0:T(8,128)}, f32[512,192]{1,0:T(8,128)}) custom-call(f32[256,192]{1,0:T(8,128)} %get-tuple-element.17.refs_0_, f32[256,192]{1,0:T(8,128)} %copy-done.2, f32[256,192]{1,0:T(8,128)} %get-tuple-element.34.refs_1_.refs_2_, s32[2,2016]{1,0:T(2,128)} %refs_2_.2, f32[512,192]{1,0:T(8,128)} %get-tuple-element.18.refs_4_, ...), custom_call_target="tpu_custom_call" | custom-call | tf_op jit(solution)/shard_map/pallas_call | solution.py:369
  76.8 0.1 collective-permute-start.4
  77.0 3.7 %shard_map.78 = (f32[128,192]{1,0:T(8,128)}, f32[128,2016]{1,0:T(8,128)}) custom-call(f32[512,192]{1,0:T(8,128)} %get-tuple-element.26.coeffs, s32[2,2016]{1,0:T(2,128)} %refs_2_.2, f32[3,512,2048]{2,1,0:T(8,128)} %get-tuple-element.20.refs_6_.grad_i.refs_5_), custom_call_target="tpu_custom_call" | custom-call | tf_op jit(solution)/shard_map/pallas_call | solution.py:369
  80.6 1.6 %copy.12 = f32[128,192]{0,1:T(8,128)} copy(f32[128,192]{1,0:T(8,128)} %get-tuple-element.31) | data formatting | bytes 196608
  82.3 2.5 %copy.14 = f32[128,2016]{0,1:T(8,128)} copy(f32[128,2016]{1,0:T(8,128)} %get-tuple-element.33) | data formatting | bytes 2064384
  84.8 0.7 copy-done.1
  85.5 8.6 %shard_map.79 = f32[128,192]{1,0:T(8,128)} custom-call(f32[256,192]{1,0:T(8,128)} %get-tuple-element.28.refs_0_, f32[256,192]{1,0:T(8,128)} %copy-done.1, s32[2,2016]{1,0:T(2,128)} %refs_2_.2, f32[512,192]{1,0:T(8,128)} %get-tuple-element.29.refs_3_, f32[3,256,2048]{2,1,0:T(8,128)} %get-tuple-element.19.refs_5_.refs_4_, ...), custom_call_target="tpu_custom_call" | custom-call | tf_op jit(solution)/shard_map/pallas_call | solution.py:369
  94.1 1.6 %copy.13 = f32[128,192]{0,1:T(8,128)} copy(f32[128,192]{1,0:T(8,128)} %shard_map.79) | data formatting | bytes 196608
  (9 shorter events, 0.0 us)
Async XLA Ops:
  1.6 18.0 %copy-start = (f32[128,192]{1,0:T(8,128)}, f32[128,192]{1,0:T(8,128)S(1)}, u32[]{:S(2)}) copy-start(f32[128,192]{1,0:T(8,128)S(1)} %copy.11.refs_2_) | copy-start | bytes 294916
  1.6 18.0 %collective-permute-start.2 = (f32[128,192]{1,0:T(8,128)S(1)}, f32[128,192]{1,0:T(8,128)S(1)}, u32[]{:S(2)}, u32[]{:S(2)}) collective-permute-start(f32[128,192]{1,0:T(8,128)S(1)} %copy.11.refs_2_), channel_id=1, source_target_pairs={{0,6},{1,7},{2,4},{3,5},{4,2},{5,3},{6,0},{7,1},{8,14},{9,15},{10,... | collective-permute-start | bytes 294920 | tf_op jit(solution)/shard_map/ppermute | solution.py:390
  6.8 12.8 %collective-permute-start.1 = (f32[128,192]{1,0:T(8,128)S(1)}, f32[128,192]{1,0:T(8,128)S(1)}, u32[]{:S(2)}, u32[]{:S(2)}) collective-permute-start(f32[128,192]{1,0:T(8,128)S(1)} %copy.11.refs_2_), channel_id=1, source_target_pairs={{0,4},{1,5},{2,6},{3,7},{4,0},{5,1},{6,2},{7,3},{8,12},{9,13},{10,... | collective-permute-start | bytes 294920 | tf_op jit(solution)/shard_map/ppermute | solution.py:390
  6.8 12.8 %collective-permute-start = (f32[128,192]{1,0:T(8,128)S(1)}, f32[128,192]{1,0:T(8,128)S(1)}, u32[]{:S(2)}, u32[]{:S(2)}) collective-permute-start(f32[128,192]{1,0:T(8,128)S(1)} %copy.11.refs_2_), channel_id=1, source_target_pairs={{0,2},{1,3},{2,0},{3,1},{4,6},{5,7},{6,4},{7,5},{8,10},{9,11},{10,... | collective-permute-start | bytes 294920 | tf_op jit(solution)/shard_map/ppermute | solution.py:390
  19.6 0.7 copy-start.3
  19.6 0.7 copy-start.4
  19.6 0.7 copy-start.5
  50.6 1.8 %collective-permute-start.3 = (f32[256,192]{1,0:T(8,128)}, f32[256,192]{1,0:T(8,128)S(1)}, u32[]{:S(2)}, u32[]{:S(2)}) collective-permute-start(f32[256,192]{1,0:T(8,128)} %get-tuple-element.17.refs_0_), channel_id=1, source_target_pairs={{0,1},{1,0},{2,3},{3,2},{4,5},{5,4},{6,7},{7,6},{8,9},{9,8},{10,11... | collective-permute-start | bytes 589832 | tf_op jit(solution)/shard_map/ppermute | solution.py:429
  52.4 0.7 copy-start.2
  76.8 7.9 %collective-permute-start.4 = (f32[256,192]{1,0:T(8,128)}, f32[256,192]{1,0:T(8,128)S(1)}, u32[]{:S(2)}, u32[]{:S(2)}) collective-permute-start(f32[256,192]{1,0:T(8,128)} %get-tuple-element.28.refs_0_), channel_id=1, source_target_pairs={{0,1},{1,0},{2,3},{3,2},{4,5},{5,4},{6,7},{7,6},{8,9},{9,8},{10,11... | collective-permute-start | bytes 589832 | tf_op jit(solution)/shard_map/ppermute | solution.py:429
  84.8 0.7 copy-start.1

commit v2 on v1

--- a/solution.py
+++ b/solution.py
@@ -14,7 +14,7 @@
 BLOCK = 128
 CHUNK = 512
 GATHER = 4
-VMEM_LIMIT = 60 * 1024 * 1024
+MIB = 1024 * 1024
 
 
 def dot(lhs, rhs, rhs_contract=0):
@@ -249,9 +249,9 @@
     describe(ctx.vec_t, ctx.inc, ctx.lat, ctx.grad_t, ctx.desc_t, ctx.self_t)
     for index, ref in enumerate(forces_t):
         put_split(ctx.vec_t, index * rows, ref[...], atoms)
-    rows = coords_i[0].shape[0]
+    rows = coords_i[0].shape[1]
     for index, ref in enumerate(coords_i):
-        put_split(ctx.vec_i, index * rows, ref[...], atoms)
+        put_split(ctx.vec_i, index * rows, ref[...].T, atoms)
     describe(ctx.vec_i, ctx.inc, ctx.lat, ctx.grad_i, ctx.desc_i, ctx.self_i)
     matern(ctx, length_ref[0])
 
@@ -320,22 +320,19 @@
 
 def desc_kernel(atoms, coeffs, pairs, grad_i, coeffs_out, out, inc, inc_t, vec):
     build_incidence(pairs, inc, inc_t)
-    put_split(vec, 0, coeffs[...], atoms)
-    coeffs_out[...] = coeffs[...]
-    count = out.shape[1]
-
-    def body(start, block):
-        lhs = vec[:, pl.ds(start, block), :].reshape(3 * block, -1)
-        for at in range(0, inc.shape[1], CHUNK):
-            end = min(at + CHUNK, count)
-            diff = dot(lhs, inc[:, at : at + CHUNK])
-            value = jnp.zeros((block, CHUNK), f32)
-            for comp in range(3):
-                grad = grad_i[comp, pl.ds(start, block), at : at + CHUNK].astype(f32)
-                value = value + grad * diff[comp * block : (comp + 1) * block]
-            out[pl.ds(start, block), at:end] = value[:, : end - at]
-
-    loop(out.shape[0], body)
+    count, rows = out.shape
+    own = coeffs[0:rows, :]
+    put_split(vec, 0, own, atoms)
+    coeffs_out[...] = own.T
+    lhs = vec[...].reshape(3 * rows, -1)
+    for at in range(0, inc.shape[1], CHUNK):
+        end = min(at + CHUNK, count)
+        diff = dot(lhs, inc[:, at : at + CHUNK])
+        value = jnp.zeros((rows, CHUNK), f32)
+        for comp in range(3):
+            grad = grad_i[comp, 0:rows, at : at + CHUNK].astype(f32)
+            value = value + grad * diff[comp * rows : (comp + 1) * rows]
+        out[at:end, :] = value.T[: end - at, :]
 
 
 def third_kernel(n_sum, atoms, in_names, scratch_names, *refs):
@@ -347,6 +344,11 @@
     resid_out = rest[n_in]
     for name, ref in zip(scratch_names, rest[n_in + 1 :]):
         setattr(ctx, name, ref)
+    own = resid_out.shape[1]
+    ctx.grad_i = ctx.grad_i.at[:, 0:own, :]
+    ctx.desc_i = ctx.desc_i.at[0:own, :]
+    ctx.diag_i = ctx.diag_i.at[0:own, :]
+    ctx.outer = ctx.outer.at[:, 0:own]
     build_incidence(pairs, ctx.inc, ctx.inc_t)
     total = parts_in[0][...]
     for ref in parts_in[1:]:
@@ -355,26 +357,31 @@
 
     def put_resid(start, block, parts):
         for comp in range(3):
-            cols = slice(comp * atoms, (comp + 1) * atoms)
-            resid_out[pl.ds(start, block), cols] = resid_in[pl.ds(start, block), cols] - parts[comp]
+            span = slice(comp * atoms, (comp + 1) * atoms)
+            resid = resid_in[pl.ds(start, block), span] - parts[comp]
+            resid_out[span, pl.ds(start, block)] = resid.T
 
     adjoint(ctx, put_resid)
 
 
-def whole(shape):
-    return pl.BlockSpec(shape, lambda *_: (0,) * len(shape))
-
-
-def call(body, ins, specs, outs, scratch):
+def call(body, limit, ins, outs, scratch):
+    vmem = pl.BlockSpec(memory_space=pltpu.VMEM)
+    smem = pl.BlockSpec(memory_space=pltpu.SMEM)
     return pl.pallas_call(
         body,
-        grid=(1,),
-        in_specs=specs,
-        out_specs=[whole(o.shape) for o in outs],
+        in_specs=[smem if x.ndim == 1 else vmem for x in ins],
+        out_specs=[vmem for _ in outs],
         out_shape=outs,
         scratch_shapes=scratch,
-        compiler_params=pltpu.CompilerParams(vmem_limit_bytes=VMEM_LIMIT),
+        compiler_params=pltpu.CompilerParams(vmem_limit_bytes=limit),
     )(*ins)
+
+
+def gather_rows(x, axis, size):
+    others = [
+        lax.ppermute(x, axis, [(i, i ^ step) for i in range(size)]) for step in range(1, size)
+    ]
+    return [x] + others
 
 
 def per_device(n_train, n_induce, train_coords, induce_coords, train_forces, atom_pairs, length_scale):
@@ -386,37 +393,38 @@
     own = induce_coords.shape[0]
     rows_i = gather * own
 
-    coords_i = [induce_coords] + [
-        lax.ppermute(induce_coords, "induce", [(i, i ^ (2 * step)) for i in range(n_induce)])
+    coords_t = gather_rows(train_coords, "train", n_train)
+    forces_t = gather_rows(train_forces, "train", n_train)
+    turned = induce_coords.T
+    coords_i = [turned] + [
+        lax.ppermute(turned, "induce", [(i, i ^ (2 * step)) for i in range(n_induce)])
         for step in range(1, gather)
     ]
-    both = jnp.concatenate([train_coords, train_forces], axis=1)
-    both = lax.all_gather(both, "train", axis=0, tiled=True)
-    coords_t = [both[:, : 3 * atoms]]
-    forces_t = [both[:, 3 * atoms :]]
-
-    grad_dtype = f32 if (rows_t + rows_i) * wide * 12 <= 20 * 1024 * 1024 else bf16
+
+    grad_dtype = f32 if (rows_t + rows_i) * wide * 12 <= 20 * MIB else bf16
     sds = jax.ShapeDtypeStruct
     kept_names = ["grad_t", "grad_i", "desc_t", "desc_i", "diag_t", "diag_i", "outer"]
     kept = [
-        sds((3, rows_t, wide), grad_dtype),
-        sds((3, rows_i, wide), grad_dtype),
-        sds((rows_t, wide), bf16),
-        sds((rows_i, wide), bf16),
-        sds((rows_t, rows_i), bf16),
-        sds((rows_i, rows_t), bf16),
-        sds((rows_t, rows_i), f32),
+        ((3, rows_t, wide), grad_dtype),
+        ((3, rows_i, wide), grad_dtype),
+        ((rows_t, wide), bf16),
+        ((rows_i, wide), bf16),
+        ((rows_t, rows_i), bf16),
+        ((rows_i, rows_t), bf16),
+        ((rows_t, rows_i), f32),
     ]
+    size = sum(math.prod(shape) * jnp.dtype(dtype).itemsize for shape, dtype in kept)
+    stays = size <= 30 * MIB and rows_t <= 256
+    limit = 24 * MIB if stays else 60 * MIB
+    kept = [(pltpu.VMEM if stays else sds)(shape, dtype) for shape, dtype in kept]
     vec_t = sds((rows_t, 3 * atoms), f32)
     vec_i = sds((rows_i, 3 * atoms), f32)
     names = ["inc", "inc_t", "lat", "vec_t", "vec_i", "vals_t", "vals_i", "self_t", "self_i"]
     names += ["sum_t", "sum_i", "cross_t", "cross_i"]
-    smem = pl.BlockSpec(memory_space=pltpu.SMEM)
-    ins = coords_t + forces_t + coords_i + [atom_pairs]
     partial, start, *state = call(
         functools.partial(first_kernel, len(coords_t), len(coords_i), atoms, kept_names, names),
-        ins + [length_scale],
-        [whole(x.shape) for x in ins] + [smem],
+        limit,
+        coords_t + forces_t + coords_i + [atom_pairs, length_scale],
         [vec_t, vec_i] + kept,
         scratch_of(rows_t, rows_i, wide, atoms, names),
     )
@@ -430,37 +438,32 @@
 
     names = [name for name in names if name != "lat"]
     parts = reduce_parts(partial)
-    ins = parts + forces_t + [atom_pairs, start] + state
     partial, coeffs, resid = call(
         functools.partial(second_kernel, len(parts), len(forces_t), atoms, kept_names, names),
-        ins,
-        [whole(x.shape) for x in ins],
+        limit,
+        parts + forces_t + [atom_pairs, start] + state,
         [vec_t, vec_i, vec_i],
         scratch_of(rows_t, rows_i, wide, atoms, names),
     )
-    own_vec = sds((own, 3 * atoms), f32)
+    parts = reduce_parts(partial)
+    own_vec = sds((3 * atoms, own), f32)
     coeffs, desc_coeffs = call(
         functools.partial(desc_kernel, atoms),
+        limit,
         [coeffs, atom_pairs, state[1]],
-        [whole(own_vec.shape), whole(atom_pairs.shape), whole((3, own, wide))],
-        [own_vec, sds((own, count), f32)],
+        [own_vec, sds((count, own), f32)],
         scratch_of(rows_t, own, wide, atoms, ["inc", "inc_t", "vec_i"]),
     )
     names = ["inc", "inc_t", "vec_t", "vals_t", "self_t", "sum_i", "cross_i"]
-    parts = reduce_parts(partial)
     in_names = ["grad_t", "grad_i", "desc_t", "desc_i", "diag_i", "outer"]
-    ins = parts + [atom_pairs, resid] + state[:4] + state[5:]
-    specs = [whole(x.shape) for x in parts + [atom_pairs]]
-    specs += [whole(own_vec.shape), whole(kept[0].shape), whole((3, own, wide)), whole(kept[2].shape)]
-    specs += [whole((own, wide)), whole((own, rows_t)), whole((rows_t, own))]
     (resid,) = call(
         functools.partial(third_kernel, len(parts), atoms, in_names, names),
-        ins,
-        specs,
+        limit,
+        parts + [atom_pairs, resid] + state[:4] + state[5:],
         [own_vec],
         scratch_of(rows_t, own, wide, atoms, names),
     )
-    return (coeffs, resid, desc_coeffs)
+    return (coeffs.T, resid.T, desc_coeffs.T)
 
 
 def solution(mesh):

time: 96.1 us -> 69 us (0.72)
  Pallas kernels: 66.2 us -> 43.5 us
  blocking collectives: 9.66 us -> 0 us
  starting transfers between devices: 5.98 us -> 13.5 us
  local copies, waits for them, and re-layouts: 9.81 us -> 4.13 us
  waiting for transfers between devices: 1.74 us -> 6.21 us
    pallas_call x4, Pallas kernels: 66.2 us -> 43.5 us  [call(): pl.pallas_call(body, in_specs=[smem if x.ndim == 1 else vmem for x in ins...]
    all_gather x1 -> x0, blocking collectives: 9.66 us -> none  [per_device(): both = lax.all_gather(both, 'train', axis=0, tiled=True)]
    ppermute x3 -> x9, starting transfers between devices: 5.78 us -> 13.2 us  [the longest x6 8.8 us: gather_rows(): lax.ppermute(x, axis, [(i, i ^ step) for i in range(size)])]
    unnamed x16 -> x10, local copies, waits for them, and re-layouts: 8.91 us -> 4.13 us
    ppermute x3 -> x9, waiting for transfers between devices: 0.01 us -> 4.68 us  [the longest x6 3.02 us: gather_rows(): lax.ppermute(x, axis, [(i, i ^ step) for i in range(size)])]
  transfers between devices with their start and end apart: 5 -> 11, of which waited for: 1 -> 4; matrix products, arithmetic and copies ran while one was open for 6% -> 0% of each run, Pallas kernels for 4% -> 2%
where the time goes in v2:
time: 69 us; the launch traced here: 68.6 us
  Pallas kernels  43.5 us (63%)
  starting transfers between devices  13.5 us (20%)
  waiting for transfers between devices  6.21 us (9%)
  local copies, waits for them, and re-layouts  4.13 us (6%)
  between operations  1.32 us (2%)
    pallas_call x4, Pallas kernels, call(): pl.pallas_call(body, in_specs=[smem if x.ndim == 1 else vmem for x in ins...  43.5 us
    ppermute x6, starting transfers between devices, gather_rows(): lax.ppermute(x, axis, [(i, i ^ step) for i in range(size)])  8.8 us
    ppermute x3, starting transfers between devices, per_device(): lax.ppermute(turned, 'induce', [(i, i ^ 2 * step) for i in range(n_induce)])  4.39 us
    unnamed x10, local copies, waits for them, and re-layouts  4.13 us
    ppermute x6, waiting for transfers between devices, gather_rows(): lax.ppermute(x, axis, [(i, i ^ step) for i in range(size)])  3.02 us
    ppermute x3, waiting for transfers between devices, per_device(): lax.ppermute(turned, 'induce', [(i, i ^ 2 * step) for i in range(n_induce)])  1.67 us
    ppermute x2, waiting for transfers between devices, reduce_parts(): return [x, lax.ppermute(x, 'induce', [(i, i ^ 1) for i in range(n_induce)])]  1.52 us
  transfers between devices with their start and end apart: 11, of which 4 were waited for; matrix products, arithmetic and copies ran while one was open for 0% of the time, Pallas kernels for 2%

profile of v2, /device:TPU:0, one launch (start us, length us, event | category | flops | bytes accessed | tf_op | source)
XLA Modules:
  0.0 68.6 jit_solution(11387221116027524981)
XLA Ops:
  0.6 3.1 %collective-permute-start.1 = (f32[64,192]{1,0:T(8,128)}, f32[64,192]{1,0:T(8,128)S(1)}, u32[]{:S(2)}, u32[]{:S(2)}) collective-permute-start(f32[64,192]{1,0:T(8,128)} %refs_0_.1), channel_id=1, source_target_pairs={{0,16},{8,24},{16,0},{24,8},{1,17},{9,25},{17,1},{25,9},{2,18},{10... | collective-permute-start | bytes 147464 | tf_op jit(solution)/shard_map/ppermute | solution.py:382
  3.7 1.5 %collective-permute-start = (f32[64,192]{1,0:T(8,128)}, f32[64,192]{1,0:T(8,128)S(1)}, u32[]{:S(2)}, u32[]{:S(2)}) collective-permute-start(f32[64,192]{1,0:T(8,128)} %refs_0_.1), channel_id=1, source_target_pairs={{0,8},{8,0},{16,24},{24,16},{1,9},{9,1},{17,25},{25,17},{2,10},{10... | collective-permute-start | bytes 147464 | tf_op jit(solution)/shard_map/ppermute | solution.py:382
  5.2 0.0 collective-permute-start.2
  5.2 2.9 %collective-permute-start.5 = (f32[64,192]{1,0:T(8,128)}, f32[64,192]{1,0:T(8,128)S(1)}, u32[]{:S(2)}, u32[]{:S(2)}) collective-permute-start(f32[64,192]{1,0:T(8,128)} %refs_2_.2), channel_id=1, source_target_pairs={{0,24},{8,16},{16,8},{24,0},{1,25},{9,17},{17,9},{25,1},{2,26},{10... | collective-permute-start | bytes 147464 | tf_op jit(solution)/shard_map/ppermute | solution.py:382
  8.1 3.6 %collective-permute-start.8 = (f32[192,128]{1,0:T(8,128)}, f32[192,128]{1,0:T(8,128)S(1)}, u32[]{:S(2)}, u32[]{:S(2)}) collective-permute-start(f32[192,128]{1,0:T(8,128)} %bitcast.4), channel_id=1, source_target_pairs={{0,6},{1,7},{2,4},{3,5},{4,2},{5,3},{6,0},{7,1},{8,14},{9,15},{10,... | collective-permute-start | bytes 294920 | tf_op jit(solution)/shard_map/ppermute | solution.py:400
  11.7 0.0 collective-permute-done.1.refs_2_
  11.7 0.8 %collective-permute-start.6 = (f32[192,128]{1,0:T(8,128)}, f32[192,128]{1,0:T(8,128)S(1)}, u32[]{:S(2)}, u32[]{:S(2)}) collective-permute-start(f32[192,128]{1,0:T(8,128)} %bitcast.6), channel_id=1, source_target_pairs={{0,2},{1,3},{2,0},{3,1},{4,6},{5,7},{6,4},{7,5},{8,10},{9,11},{10,... | collective-permute-start | bytes 294920 | tf_op jit(solution)/shard_map/ppermute | solution.py:400
  12.5 0.5 collective-permute-start.4
  13.0 0.8 %collective-permute-start.3 = (f32[64,192]{1,0:T(8,128)}, f32[64,192]{1,0:T(8,128)S(1)}, u32[]{:S(2)}, u32[]{:S(2)}) collective-permute-start(f32[64,192]{1,0:T(8,128)} %refs_2_.2), channel_id=1, source_target_pairs={{0,8},{8,0},{16,24},{24,16},{1,9},{9,1},{17,25},{25,17},{2,10},{10... | collective-permute-start | bytes 147464 | tf_op jit(solution)/shard_map/ppermute | solution.py:382
  14.5 2.5 %collective-permute-done.4.refs_6_.refs_4_ = f32[64,192]{1,0:T(8,128)S(1)} collective-permute-done((f32[64,192]{1,0:T(8,128)}, f32[64,192]{1,0:T(8,128)S(1)}, u32[]{:S(2)}, u32[]{:S(2)}) %collective-permute-start.4) | collective-permute-done | bytes 49184 | tf_op jit(solution)/shard_map/ppermute | solution.py:382
  17.0 0.5 collective-permute-done.3.refs_5_.refs_3_
  17.5 1.7 %collective-permute-done.7.refs_10_ = f32[192,128]{1,0:T(8,128)S(1)} collective-permute-done((f32[192,128]{1,0:T(8,128)}, f32[192,128]{1,0:T(8,128)S(1)}, u32[]{:S(2)}, u32[]{:S(2)}) %collective-permute-start.7) | collective-permute-done | bytes 98336 | tf_op jit(solution)/shard_map/ppermute | solution.py:400
  19.2 0.8 %copy-done = f32[64,192]{1,0:T(8,128)S(1)} copy-done((f32[64,192]{1,0:T(8,128)S(1)}, f32[64,192]{1,0:T(8,128)}, u32[]{:S(2)}) %copy-start) | copy-done | bytes 49176
  20.0 0.7 %copy-done.2 = s32[2,2016]{1,0:T(2,128)S(1)} copy-done((s32[2,2016]{1,0:T(2,128)S(1)}, s32[2,2016]{1,0:T(2,128)}, u32[]{:S(2)}) %copy-start.2) | copy-done | bytes 16152
  20.7 0.9 %copy-done.3 = f32[128,192]{0,1:T(8,128)S(1)} copy-done((f32[128,192]{0,1:T(8,128)S(1)}, f32[128,192]{0,1:T(8,128)}, u32[]{:S(2)}) %copy-start.3) | copy-done | bytes 98328
  21.6 0.8 %copy-done.4 = f32[64,192]{1,0:T(8,128)S(1)} copy-done((f32[64,192]{1,0:T(8,128)S(1)}, f32[64,192]{1,0:T(8,128)}, u32[]{:S(2)}) %copy-start.4) | copy-done | bytes 49176
  22.5 22.3 %shard_map.76 = (f32[256,192]{1,0:T(8,128)S(1)}, f32[512,192]{1,0:T(8,128)S(1)}, f32[3,256,2048]{2,1,0:T(8,128)S(1)}, f32[3,512,2048]{2,1,0:T(8,128)S(1)}, bf16[...) custom-call(f32[64,192]{1,0:T(8,128)S(1)} %copy-done.4, ...), custom_call_target="tpu_custom_call" | custom-call | tf_op jit(solution)/shard_map/pallas_call | solution.py:370
  44.7 0.1 collective-permute-start.9
  44.8 1.5 %collective-permute-done.9.refs_1_ = f32[256,192]{1,0:T(8,128)S(1)} collective-permute-done((f32[256,192]{1,0:T(8,128)S(1)}, f32[256,192]{1,0:T(8,128)S(1)}, u32[]{:S(2)}, u32[]{:S(2)}) %collective-permute-start.9) | collective-permute-done | bytes 196640 | tf_op jit(solution)/shard_map/ppermute | solution.py:437
  46.3 0.8 %copy-done.1 = f32[64,192]{1,0:T(8,128)S(1)} copy-done((f32[64,192]{1,0:T(8,128)S(1)}, f32[64,192]{1,0:T(8,128)}, u32[]{:S(2)}) %copy-start.1) | copy-done | bytes 49176
  47.2 15.2 %shard_map.77 = (f32[256,192]{1,0:T(8,128)S(1)}, f32[512,192]{1,0:T(8,128)S(1)}, f32[512,192]{1,0:T(8,128)S(1)}) custom-call(f32[256,192]{1,0:T(8,128)S(1)} %get-tuple-element.17.refs_0_, f32[256,192]{1,0:T(8,128)S(1)} %collective-permute-done.9.refs_1_, f32[64,192]{1,0:T(8,128)S(1)} %copy-done.1, f32[64,192]{1,0:T(8,128)S(1)} %collective-permute-done.3.refs_5_.refs_3_, ...), custom_call_target="tpu_custom_call" | custom-call | tf_op jit(solution)/shard_map/pallas_call | solution.py:370
  62.3 0.2 collective-permute-start.10
  62.5 1.7 %shard_map.78 = (f32[192,128]{1,0:T(8,128)}, f32[2016,128]{1,0:T(8,128)}) custom-call(f32[512,192]{1,0:T(8,128)S(1)} %get-tuple-element.26.coeffs, s32[2,2016]{1,0:T(2,128)S(1)} %copy-done.2, f32[3,512,2048]{2,1,0:T(8,128)S(1)} %get-tuple-element.20.refs_9_.grad_i.refs_5_), custom_call_target="tpu_custom_call" | custom-call | tf_op jit(solution)/shard_map/pallas_call | solution.py:370
  64.3 4.4 %shard_map.79 = f32[192,128]{1,0:T(8,128)} custom-call(f32[256,192]{1,0:T(8,128)S(1)} %get-tuple-element.28.refs_0_, f32[256,192]{1,0:T(8,128)S(1)} %collective-permute-done.10.refs_1_, s32[2,2016]{1,0:T(2,128)S(1)} %copy-done.2, f32[512,192]{1,0:T(8,128)S(1)} %get-tuple-element.29.refs_3_, f32[3,256,2048]{2,1,0:T(8,128)S(1)} %get-tuple-element.19.refs_8_.refs_4_, ...), custom_call_target="tpu_custom_call" | custom-call | tf_op jit(solution)/shard_map/pallas_call | solution.py:370
  (12 shorter events, 0.0 us)
Async XLA Ops:
  0.6 11.1 %collective-permute-start.1 = (f32[64,192]{1,0:T(8,128)}, f32[64,192]{1,0:T(8,128)S(1)}, u32[]{:S(2)}, u32[]{:S(2)}) collective-permute-start(f32[64,192]{1,0:T(8,128)} %refs_0_.1), channel_id=1, source_target_pairs={{0,16},{8,24},{16,0},{24,8},{1,17},{9,25},{17,1},{25,9},{2,18},{10... | collective-permute-start | bytes 147464 | tf_op jit(solution)/shard_map/ppermute | solution.py:382
  3.7 8.0 %collective-permute-start = (f32[64,192]{1,0:T(8,128)}, f32[64,192]{1,0:T(8,128)S(1)}, u32[]{:S(2)}, u32[]{:S(2)}) collective-permute-start(f32[64,192]{1,0:T(8,128)} %refs_0_.1), channel_id=1, source_target_pairs={{0,8},{8,0},{16,24},{24,16},{1,9},{9,1},{17,25},{25,17},{2,10},{10... | collective-permute-start | bytes 147464 | tf_op jit(solution)/shard_map/ppermute | solution.py:382
  5.2 7.3 %collective-permute-start.2 = (f32[64,192]{1,0:T(8,128)}, f32[64,192]{1,0:T(8,128)S(1)}, u32[]{:S(2)}, u32[]{:S(2)}) collective-permute-start(f32[64,192]{1,0:T(8,128)} %refs_0_.1), channel_id=1, source_target_pairs={{0,24},{8,16},{16,8},{24,0},{1,25},{9,17},{17,9},{25,1},{2,26},{10... | collective-permute-start | bytes 147464 | tf_op jit(solution)/shard_map/ppermute | solution.py:382
  5.2 7.8 %collective-permute-start.5 = (f32[64,192]{1,0:T(8,128)}, f32[64,192]{1,0:T(8,128)S(1)}, u32[]{:S(2)}, u32[]{:S(2)}) collective-permute-start(f32[64,192]{1,0:T(8,128)} %refs_2_.2), channel_id=1, source_target_pairs={{0,24},{8,16},{16,8},{24,0},{1,25},{9,17},{17,9},{25,1},{2,26},{10... | collective-permute-start | bytes 147464 | tf_op jit(solution)/shard_map/ppermute | solution.py:382
  8.1 9.4 %collective-permute-start.8 = (f32[192,128]{1,0:T(8,128)}, f32[192,128]{1,0:T(8,128)S(1)}, u32[]{:S(2)}, u32[]{:S(2)}) collective-permute-start(f32[192,128]{1,0:T(8,128)} %bitcast.4), channel_id=1, source_target_pairs={{0,6},{1,7},{2,4},{3,5},{4,2},{5,3},{6,0},{7,1},{8,14},{9,15},{10,... | collective-permute-start | bytes 294920 | tf_op jit(solution)/shard_map/ppermute | solution.py:400
  11.7 7.4 %collective-permute-start.7 = (f32[192,128]{1,0:T(8,128)}, f32[192,128]{1,0:T(8,128)S(1)}, u32[]{:S(2)}, u32[]{:S(2)}) collective-permute-start(f32[192,128]{1,0:T(8,128)} %bitcast.5), channel_id=1, source_target_pairs={{0,4},{1,5},{2,6},{3,7},{4,0},{5,1},{6,2},{7,3},{8,12},{9,13},{10,... | collective-permute-start | bytes 294920 | tf_op jit(solution)/shard_map/ppermute | solution.py:400
  11.7 7.4 %collective-permute-start.6 = (f32[192,128]{1,0:T(8,128)}, f32[192,128]{1,0:T(8,128)S(1)}, u32[]{:S(2)}, u32[]{:S(2)}) collective-permute-start(f32[192,128]{1,0:T(8,128)} %bitcast.6), channel_id=1, source_target_pairs={{0,2},{1,3},{2,0},{3,1},{4,6},{5,7},{6,4},{7,5},{8,10},{9,11},{10,... | collective-permute-start | bytes 294920 | tf_op jit(solution)/shard_map/ppermute | solution.py:400
  12.5 4.5 %collective-permute-start.4 = (f32[64,192]{1,0:T(8,128)}, f32[64,192]{1,0:T(8,128)S(1)}, u32[]{:S(2)}, u32[]{:S(2)}) collective-permute-start(f32[64,192]{1,0:T(8,128)} %refs_2_.2), channel_id=1, source_target_pairs={{0,16},{8,24},{16,0},{24,8},{1,17},{9,25},{17,1},{25,9},{2,18},{10... | collective-permute-start | bytes 147464 | tf_op jit(solution)/shard_map/ppermute | solution.py:382
  13.0 4.5 %collective-permute-start.3 = (f32[64,192]{1,0:T(8,128)}, f32[64,192]{1,0:T(8,128)S(1)}, u32[]{:S(2)}, u32[]{:S(2)}) collective-permute-start(f32[64,192]{1,0:T(8,128)} %refs_2_.2), channel_id=1, source_target_pairs={{0,8},{8,0},{16,24},{24,16},{1,9},{9,1},{17,25},{25,17},{2,10},{10... | collective-permute-start | bytes 147464 | tf_op jit(solution)/shard_map/ppermute | solution.py:382
  19.2 0.8 %copy-start = (f32[64,192]{1,0:T(8,128)S(1)}, f32[64,192]{1,0:T(8,128)}, u32[]{:S(2)}) copy-start(f32[64,192]{1,0:T(8,128)} %refs_2_.2) | copy-start | bytes 147460
  20.0 0.7 %copy-start.2 = (s32[2,2016]{1,0:T(2,128)S(1)}, s32[2,2016]{1,0:T(2,128)}, u32[]{:S(2)}) copy-start(s32[2,2016]{1,0:T(2,128)} %refs_2_.3) | copy-start | bytes 48388
  20.7 0.9 %copy-start.3 = (f32[128,192]{0,1:T(8,128)S(1)}, f32[128,192]{0,1:T(8,128)}, u32[]{:S(2)}) copy-start(f32[128,192]{0,1:T(8,128)} %param.6) | copy-start | bytes 294916
  21.6 0.8 %copy-start.4 = (f32[64,192]{1,0:T(8,128)S(1)}, f32[64,192]{1,0:T(8,128)}, u32[]{:S(2)}) copy-start(f32[64,192]{1,0:T(8,128)} %refs_0_.1) | copy-start | bytes 147460
  44.7 1.6 %collective-permute-start.9 = (f32[256,192]{1,0:T(8,128)S(1)}, f32[256,192]{1,0:T(8,128)S(1)}, u32[]{:S(2)}, u32[]{:S(2)}) collective-permute-start(f32[256,192]{1,0:T(8,128)S(1)} %get-tuple-element.17.refs_0_), channel_id=1, source_target_pairs={{0,1},{1,0},{2,3},{3,2},{4,5},{5,4},{6,7},{7,6},{8,9},{9,8},{10,11... | collective-permute-start | bytes 589832 | tf_op jit(solution)/shard_map/ppermute | solution.py:437
  46.3 0.8 %copy-start.1 = (f32[64,192]{1,0:T(8,128)S(1)}, f32[64,192]{1,0:T(8,128)}, u32[]{:S(2)}) copy-start(f32[64,192]{1,0:T(8,128)} %refs_2_.2) | copy-start | bytes 147460
  62.3 1.9 %collective-permute-start.10 = (f32[256,192]{1,0:T(8,128)S(1)}, f32[256,192]{1,0:T(8,128)S(1)}, u32[]{:S(2)}, u32[]{:S(2)}) collective-permute-start(f32[256,192]{1,0:T(8,128)S(1)} %get-tuple-element.28.refs_0_), channel_id=1, source_target_pairs={{0,1},{1,0},{2,3},{3,2},{4,5},{5,4},{6,7},{7,6},{8,9},{9,8},{10,11... | collective-permute-start | bytes 589832 | tf_op jit(solution)/shard_map/ppermute | solution.py:437

commit v3 on v2

--- a/solution.py
+++ b/solution.py
@@ -11,8 +11,10 @@
 root_five = math.sqrt(5.0)
 f32 = jnp.float32
 bf16 = jnp.bfloat16
-BLOCK = 128
-CHUNK = 512
+CHUNK = 256
+DESCRIBE_BLOCK = 256
+DESC_BLOCK = 256
+MIX_BLOCK = 512
 GATHER = 4
 MIB = 1024 * 1024
 
@@ -63,8 +65,8 @@
     return lax.rsqrt(total + padding)[0:1, :], padding[0:1, :]
 
 
-def loop(rows, body):
-    block = min(rows, BLOCK)
+def loop(rows, block, body):
+    block = min(rows, block)
     if rows == block:
         body(0, block)
         return
@@ -102,7 +104,7 @@
             jnp.sum(sq, axis=1, keepdims=True), (block, 128)
         )
 
-    loop(rows, body)
+    loop(rows, DESCRIBE_BLOCK, body)
 
 
 def to_desc(split_ref, inc_ref, grad_ref, desc_ref, out_ref, self_ref):
@@ -127,7 +129,7 @@
             jnp.sum(total, axis=1, keepdims=True), (block, 128)
         )
 
-    loop(rows, body)
+    loop(rows, DESC_BLOCK, body)
 
 
 def mix_to_forces(diag_ref, vals_ref, cross_ref, desc_ref, own_ref, sum_ref, grad_ref, inc_t_ref, put):
@@ -151,7 +153,7 @@
             forces = part if forces is None else forces + part
         put(start, block, [forces[c * block : (c + 1) * block] for c in range(3)])
 
-    loop(rows, body)
+    loop(rows, MIX_BLOCK, body)
 
 
 def lane_sum(x):
@@ -159,7 +161,6 @@
 
 
 def adjoint(ctx, put):
-    to_desc(ctx.vec_t, ctx.inc, ctx.grad_t, ctx.desc_t, ctx.vals_t, ctx.self_t)
     rows = ctx.desc_t.shape[0]
     block = min(rows, 256)
     for at in range(0, rows, block):
@@ -197,7 +198,7 @@
     for at in range(0, rows, block):
         span = slice(at, at + block)
         inner = dot(ctx.desc_t[span, :], ctx.desc_i[...], 1)
-        square = ctx.self_t[span, 0:1] + col_sq - 2.0 * inner
+        square = ctx.sq_t[span, 0:1] + col_sq - 2.0 * inner
         radius = root_five * (jnp.sqrt(jnp.maximum(square, 0.0)) / length)
         falloff = jnp.exp(-radius)
         diag = 5.0 / (3.0 * length**2) * (1.0 + radius) * falloff
@@ -231,24 +232,45 @@
     return [pltpu.VMEM(*kinds[name]) for name in names]
 
 
-def first_kernel(n_train, n_induce, atoms, out_names, scratch_names, *refs):
-    coords_t = refs[:n_train]
-    forces_t = refs[n_train : 2 * n_train]
-    coords_i = refs[2 * n_train : 2 * n_train + n_induce]
-    pairs, length_ref = refs[2 * n_train + n_induce : 2 * n_train + n_induce + 2]
-    rest = refs[2 * n_train + n_induce + 2 :]
-    partial, start_out = rest[:2]
-    ctx = Ctx(out_names + scratch_names, rest[2:])
+def join_kernel(coords, forces, turned, pairs, both_out, turned_out, pairs_out, left, right, sems):
+    width = coords.shape[1]
+    copies = [
+        pltpu.make_async_copy(source, target, sems.at[index])
+        for index, (source, target) in enumerate(
+            ((coords, left), (forces, right), (turned, turned_out), (pairs, pairs_out))
+        )
+    ]
+    for copy in copies:
+        copy.start()
+    for copy in copies:
+        copy.wait()
+    both_out[:, :width] = left[...]
+    both_out[:, width:] = right[...]
+
+
+def train_kernel(n_train, atoms, out_names, *refs):
+    both_t = refs[:n_train]
+    pairs = refs[n_train]
+    ctx = Ctx(out_names + ["vec_t"], refs[n_train + 1 :])
     build_incidence(pairs, ctx.inc, ctx.inc_t)
     lattice, padding = lattice_inverse(ctx.inc, atoms, pairs.shape[1])
     ctx.lat[0:1, :] = lattice
     ctx.lat[1:2, :] = padding
-    rows = coords_t[0].shape[0]
-    for index, ref in enumerate(coords_t):
-        put_split(ctx.vec_t, index * rows, ref[...], atoms)
-    describe(ctx.vec_t, ctx.inc, ctx.lat, ctx.grad_t, ctx.desc_t, ctx.self_t)
-    for index, ref in enumerate(forces_t):
-        put_split(ctx.vec_t, index * rows, ref[...], atoms)
+    rows = both_t[0].shape[0]
+    for index, ref in enumerate(both_t):
+        put_split(ctx.vec_t, index * rows, ref[:, : 3 * atoms], atoms)
+    describe(ctx.vec_t, ctx.inc, ctx.lat, ctx.grad_t, ctx.desc_t, ctx.sq_t)
+    for index, ref in enumerate(both_t):
+        put_split(ctx.vec_t, index * rows, ref[:, 3 * atoms :], atoms)
+    to_desc(ctx.vec_t, ctx.inc, ctx.grad_t, ctx.desc_t, ctx.vals_t, ctx.self_t)
+
+
+def first_kernel(n_induce, atoms, in_names, out_names, scratch_names, *refs):
+    coords_i = refs[:n_induce]
+    length_ref = refs[n_induce]
+    n_in = n_induce + 1 + len(in_names)
+    partial, start_out = refs[n_in : n_in + 2]
+    ctx = Ctx(in_names + out_names + scratch_names, refs[n_induce + 1 : n_in] + refs[n_in + 2 :])
     rows = coords_i[0].shape[1]
     for index, ref in enumerate(coords_i):
         put_split(ctx.vec_i, index * rows, ref[...].T, atoms)
@@ -271,16 +293,15 @@
 
 def second_kernel(n_sum, n_train, atoms, in_names, scratch_names, *refs):
     parts_in = refs[:n_sum]
-    forces_t = refs[n_sum : n_sum + n_train]
+    both_t = refs[n_sum : n_sum + n_train]
     rest = refs[n_sum + n_train :]
-    pairs, start_in = rest[:2]
+    start_in = rest[0]
     n_in = len(in_names)
-    ctx = Ctx(in_names, rest[2 : 2 + n_in])
-    partial, coeffs_out, resid_out = rest[2 + n_in : 5 + n_in]
-    for name, ref in zip(scratch_names, rest[5 + n_in :]):
+    ctx = Ctx(in_names, rest[1 : 1 + n_in])
+    partial, coeffs_out, resid_out = rest[1 + n_in : 4 + n_in]
+    for name, ref in zip(scratch_names, rest[4 + n_in :]):
         setattr(ctx, name, ref)
-    build_incidence(pairs, ctx.inc, ctx.inc_t)
-    rows = forces_t[0].shape[0]
+    rows = both_t[0].shape[0]
     probed_sq = jnp.zeros((1, 1), f32)
     cross_sq = jnp.zeros((1, 1), f32)
     for index in range(n_train):
@@ -290,7 +311,7 @@
             probed = probed + ref[span, :]
         put_split(ctx.vec_t, index * rows, probed, atoms)
         probed_sq = probed_sq + jnp.sum(probed * probed, keepdims=True)
-        cross_sq = cross_sq + jnp.sum(forces_t[index][...] * probed, keepdims=True)
+        cross_sq = cross_sq + jnp.sum(both_t[index][:, 3 * atoms :] * probed, keepdims=True)
     quotient = probed_sq / cross_sq
     center = 0.775 * quotient
     spread = 0.725 * quotient
@@ -309,6 +330,7 @@
             coeffs_out[pl.ds(start, block), cols] = coeffs + direction
             ctx.vec_i[comp, pl.ds(start, block), :] = split_three(direction)
 
+    to_desc(ctx.vec_t, ctx.inc, ctx.grad_t, ctx.desc_t, ctx.vals_t, ctx.self_t)
     adjoint(ctx, put_resid)
 
     def put_partial(start, block, parts):
@@ -318,8 +340,7 @@
     forward(ctx, put_partial)
 
 
-def desc_kernel(atoms, coeffs, pairs, grad_i, coeffs_out, out, inc, inc_t, vec):
-    build_incidence(pairs, inc, inc_t)
+def desc_kernel(atoms, coeffs, inc, grad_i, coeffs_out, out, vec):
     count, rows = out.shape
     own = coeffs[0:rows, :]
     put_split(vec, 0, own, atoms)
@@ -337,9 +358,9 @@
 
 def third_kernel(n_sum, atoms, in_names, scratch_names, *refs):
     parts_in = refs[:n_sum]
-    pairs, resid_in = refs[n_sum : n_sum + 2]
+    resid_in = refs[n_sum]
     n_in = len(in_names)
-    rest = refs[n_sum + 2 :]
+    rest = refs[n_sum + 1 :]
     ctx = Ctx(in_names, rest[:n_in])
     resid_out = rest[n_in]
     for name, ref in zip(scratch_names, rest[n_in + 1 :]):
@@ -349,7 +370,6 @@
     ctx.desc_i = ctx.desc_i.at[0:own, :]
     ctx.diag_i = ctx.diag_i.at[0:own, :]
     ctx.outer = ctx.outer.at[:, 0:own]
-    build_incidence(pairs, ctx.inc, ctx.inc_t)
     total = parts_in[0][...]
     for ref in parts_in[1:]:
         total = total + ref[...]
@@ -361,15 +381,17 @@
             resid = resid_in[pl.ds(start, block), span] - parts[comp]
             resid_out[span, pl.ds(start, block)] = resid.T
 
+    to_desc(ctx.vec_t, ctx.inc, ctx.grad_t, ctx.desc_t, ctx.vals_t, ctx.self_t)
     adjoint(ctx, put_resid)
 
 
-def call(body, limit, ins, outs, scratch):
+def call(body, limit, ins, outs, scratch, fetch=False):
     vmem = pl.BlockSpec(memory_space=pltpu.VMEM)
     smem = pl.BlockSpec(memory_space=pltpu.SMEM)
+    hbm = pl.BlockSpec(memory_space=pl.ANY)
     return pl.pallas_call(
         body,
-        in_specs=[smem if x.ndim == 1 else vmem for x in ins],
+        in_specs=[hbm if fetch else smem if x.ndim == 1 else vmem for x in ins],
         out_specs=[vmem for _ in outs],
         out_shape=outs,
         scratch_shapes=scratch,
@@ -392,56 +414,82 @@
     rows_t = n_train * train_coords.shape[0]
     own = induce_coords.shape[0]
     rows_i = gather * own
-
-    coords_t = gather_rows(train_coords, "train", n_train)
-    forces_t = gather_rows(train_forces, "train", n_train)
-    turned = induce_coords.T
+    grad_dtype = f32 if (rows_t + rows_i) * wide * 12 <= 20 * MIB else bf16
+    kinds = dict(
+        grad_t=((3, rows_t, wide), grad_dtype),
+        grad_i=((3, rows_i, wide), grad_dtype),
+        desc_t=((rows_t, wide), bf16),
+        desc_i=((rows_i, wide), bf16),
+        diag_t=((rows_t, rows_i), bf16),
+        diag_i=((rows_i, rows_t), bf16),
+        outer=((rows_t, rows_i), f32),
+        inc=((3 * atoms, wide), bf16),
+        inc_t=((wide, atoms), bf16),
+        lat=((8, wide), f32),
+        vals_t=((rows_t, wide), bf16),
+        sq_t=((rows_t, 128), f32),
+        self_t=((rows_t, 128), f32),
+    )
+    size = sum(math.prod(shape) * jnp.dtype(dtype).itemsize for shape, dtype in kinds.values())
+    stays = size <= 32 * MIB and rows_t <= 256
+    limit = 24 * MIB if stays else 60 * MIB
+    sds = jax.ShapeDtypeStruct
+    kept = pltpu.VMEM if stays else sds
+
+    def pin(xs):
+        return [pltpu.with_memory_space_constraint(x, pltpu.VMEM) for x in xs] if stays else xs
+
+    both, turned, pairs = call(
+        join_kernel,
+        limit,
+        [train_coords, train_forces, induce_coords.T, atom_pairs],
+        [kept((train_coords.shape[0], 6 * atoms), f32), kept((3 * atoms, own), f32), kept(atom_pairs.shape, atom_pairs.dtype)],
+        [pltpu.VMEM(train_coords.shape, f32)] * 2 + [pltpu.SemaphoreType.DMA((4,))],
+        fetch=True,
+    )
+    both_t = gather_rows(both, "train", n_train)
     coords_i = [turned] + [
         lax.ppermute(turned, "induce", [(i, i ^ (2 * step)) for i in range(n_induce)])
         for step in range(1, gather)
     ]
-
-    grad_dtype = f32 if (rows_t + rows_i) * wide * 12 <= 20 * MIB else bf16
-    sds = jax.ShapeDtypeStruct
-    kept_names = ["grad_t", "grad_i", "desc_t", "desc_i", "diag_t", "diag_i", "outer"]
-    kept = [
-        ((3, rows_t, wide), grad_dtype),
-        ((3, rows_i, wide), grad_dtype),
-        ((rows_t, wide), bf16),
-        ((rows_i, wide), bf16),
-        ((rows_t, rows_i), bf16),
-        ((rows_i, rows_t), bf16),
-        ((rows_t, rows_i), f32),
-    ]
-    size = sum(math.prod(shape) * jnp.dtype(dtype).itemsize for shape, dtype in kept)
-    stays = size <= 30 * MIB and rows_t <= 256
-    limit = 24 * MIB if stays else 60 * MIB
-    kept = [(pltpu.VMEM if stays else sds)(shape, dtype) for shape, dtype in kept]
+    both_t = both_t[:1] + pin(both_t[1:])
+    coords_i = coords_i[:1] + pin(coords_i[1:])
+
+    train_names = ["grad_t", "desc_t", "inc", "inc_t", "lat", "vals_t", "sq_t", "self_t"]
+    train_state = call(
+        functools.partial(train_kernel, n_train, atoms, train_names),
+        limit,
+        both_t + [pairs],
+        [kept(*kinds[name]) for name in train_names],
+        scratch_of(rows_t, rows_i, wide, atoms, ["vec_t"]),
+    )
+    induce_names = ["grad_i", "desc_i", "diag_t", "diag_i", "outer"]
+    names = ["vec_i", "vals_i", "self_i", "sum_t", "sum_i", "cross_t", "cross_i"]
     vec_t = sds((rows_t, 3 * atoms), f32)
     vec_i = sds((rows_i, 3 * atoms), f32)
-    names = ["inc", "inc_t", "lat", "vec_t", "vec_i", "vals_t", "vals_i", "self_t", "self_i"]
-    names += ["sum_t", "sum_i", "cross_t", "cross_i"]
-    partial, start, *state = call(
-        functools.partial(first_kernel, len(coords_t), len(coords_i), atoms, kept_names, names),
+    partial, start, *induce_state = call(
+        functools.partial(first_kernel, gather, atoms, train_names, induce_names, names),
         limit,
-        coords_t + forces_t + coords_i + [atom_pairs, length_scale],
-        [vec_t, vec_i] + kept,
+        coords_i + [length_scale] + list(train_state),
+        [vec_t, vec_i] + [kept(*kinds[name]) for name in induce_names],
         scratch_of(rows_t, rows_i, wide, atoms, names),
     )
+    kept_names = ["grad_t", "desc_t", "inc", "inc_t"] + induce_names
+    state = list(train_state[:4]) + list(induce_state)
 
     def reduce_parts(x):
         step = 2 * gather
         while step < n_induce:
             x = x + lax.ppermute(x, "induce", [(i, i ^ step) for i in range(n_induce)])
             step *= 2
-        return [x, lax.ppermute(x, "induce", [(i, i ^ 1) for i in range(n_induce)])]
-
-    names = [name for name in names if name != "lat"]
+        return pin([x, lax.ppermute(x, "induce", [(i, i ^ 1) for i in range(n_induce)])])
+
+    names = ["vec_t", "vals_t", "self_t"] + names
     parts = reduce_parts(partial)
     partial, coeffs, resid = call(
-        functools.partial(second_kernel, len(parts), len(forces_t), atoms, kept_names, names),
+        functools.partial(second_kernel, len(parts), n_train, atoms, kept_names, names),
         limit,
-        parts + forces_t + [atom_pairs, start] + state,
+        parts + both_t + [start] + state,
         [vec_t, vec_i, vec_i],
         scratch_of(rows_t, rows_i, wide, atoms, names),
     )
@@ -450,16 +498,16 @@
     coeffs, desc_coeffs = call(
         functools.partial(desc_kernel, atoms),
         limit,
-        [coeffs, atom_pairs, state[1]],
+        [coeffs, state[2], state[4]],
         [own_vec, sds((count, own), f32)],
-        scratch_of(rows_t, own, wide, atoms, ["inc", "inc_t", "vec_i"]),
-    )
-    names = ["inc", "inc_t", "vec_t", "vals_t", "self_t", "sum_i", "cross_i"]
-    in_names = ["grad_t", "grad_i", "desc_t", "desc_i", "diag_i", "outer"]
+        scratch_of(rows_t, own, wide, atoms, ["vec_i"]),
+    )
+    names = ["vec_t", "vals_t", "self_t", "sum_i", "cross_i"]
+    in_names = kept_names
     (resid,) = call(
         functools.partial(third_kernel, len(parts), atoms, in_names, names),
         limit,
-        parts + [atom_pairs, resid] + state[:4] + state[5:],
+        parts + [resid] + state,
         [own_vec],
         scratch_of(rows_t, own, wide, atoms, names),
     )

time: 69 us -> 56 us (0.81)
  Pallas kernels: 43.5 us -> 37.2 us
  starting transfers between devices: 13.5 us -> 9.47 us
  waiting for transfers between devices: 6.21 us -> 4.37 us
  local copies, waits for them, and re-layouts: 4.13 us -> 3.28 us
    pallas_call x4 -> x6, Pallas kernels: 43.5 us -> 37.2 us  [call(): pl.pallas_call(body, in_specs=[hbm if fetch else smem if x.ndim == 1 else...]
    ppermute x6 -> x3, starting transfers between devices: 8.8 us -> 4.63 us  [gather_rows(): lax.ppermute(x, axis, [(i, i ^ step) for i in range(size)])]
    ppermute x6 -> x3, waiting for transfers between devices: 3.02 us -> 0.01 us  [gather_rows(): lax.ppermute(x, axis, [(i, i ^ step) for i in range(size)])]
    ppermute x3, waiting for transfers between devices: 1.67 us -> 2.84 us  [per_device(): lax.ppermute(turned, 'induce', [(i, i ^ 2 * step) for i in range(n_induce)])]
    unnamed x10 -> x8, local copies, waits for them, and re-layouts: 4.13 us -> 3.28 us
  transfers between devices with their start and end apart: 11 -> 8, of which waited for: 4 -> 2; matrix products, arithmetic and copies ran while one was open for 0% -> 0% of each run, Pallas kernels for 2% -> 9%
where the time goes in v3:
time: 56 us; the launch traced here: 55.7 us
  Pallas kernels  37.2 us (66%)
  starting transfers between devices  9.47 us (17%)
  waiting for transfers between devices  4.37 us (8%)
  local copies, waits for them, and re-layouts  3.28 us (6%)
  between operations  1.35 us (2%)
    pallas_call x6, Pallas kernels, call(): pl.pallas_call(body, in_specs=[hbm if fetch else smem if x.ndim == 1 else...  37.2 us
    ppermute x3, starting transfers between devices, gather_rows(): lax.ppermute(x, axis, [(i, i ^ step) for i in range(size)])  4.63 us
    ppermute x3, starting transfers between devices, per_device(): lax.ppermute(turned, 'induce', [(i, i ^ 2 * step) for i in range(n_induce)])  4.57 us
    unnamed x8, local copies, waits for them, and re-layouts  3.28 us
    ppermute x3, waiting for transfers between devices, per_device(): lax.ppermute(turned, 'induce', [(i, i ^ 2 * step) for i in range(n_induce)])  2.84 us
    ppermute x2, waiting for transfers between devices, reduce_parts(): lax.ppermute(x, 'induce', [(i, i ^ 1) for i in range(n_induce)])  1.52 us
  transfers between devices with their start and end apart: 8, of which 2 were waited for; matrix products, arithmetic and copies ran while one was open for 0% of the time, Pallas kernels for 9%

profile of v3, /device:TPU:0, one launch (start us, length us, event | category | flops | bytes accessed | tf_op | source)
XLA Modules:
  0.0 55.7 jit_solution(2814010400747720682)
XLA Ops:
  0.6 0.9 %copy-done = f32[128,192]{0,1:T(8,128)S(1)} copy-done((f32[128,192]{0,1:T(8,128)S(1)}, f32[128,192]{0,1:T(8,128)}, u32[]{:S(2)}) %copy-start) | copy-done | bytes 98328
  1.5 0.8 %copy-done.1 = f32[64,192]{1,0:T(8,128)S(1)} copy-done((f32[64,192]{1,0:T(8,128)S(1)}, f32[64,192]{1,0:T(8,128)}, u32[]{:S(2)}) %copy-start.1) | copy-done | bytes 49176
  2.4 0.8 %copy-done.2 = f32[64,192]{1,0:T(8,128)S(1)} copy-done((f32[64,192]{1,0:T(8,128)S(1)}, f32[64,192]{1,0:T(8,128)}, u32[]{:S(2)}) %copy-start.2) | copy-done | bytes 49176
  3.2 0.7 %copy-done.3 = s32[2,2016]{1,0:T(2,128)S(1)} copy-done((s32[2,2016]{1,0:T(2,128)S(1)}, s32[2,2016]{1,0:T(2,128)}, u32[]{:S(2)}) %copy-start.3) | copy-done | bytes 16152
  3.9 0.4 shard_map.76
  4.3 4.0 %collective-permute-start.5 = (f32[64,384]{1,0:T(8,128)S(1)}, f32[64,384]{1,0:T(8,128)S(1)}, u32[]{:S(2)}, u32[]{:S(2)}) collective-permute-start(f32[64,384]{1,0:T(8,128)S(1)} %get-tuple-element.27.refs_0_.refs_2_), channel_id=1, source_target_pairs={{0,24},{8,16},{16,8},{24,0},{1,25},{9,17},{17,9},{25,1},{2,26},{10... | collective-permute-start | bytes 294920 | tf_op jit(solution)/shard_map/ppermute | solution.py:404
  8.3 0.5 collective-permute-start.4
  8.8 0.1 collective-permute-start.3
  9.0 4.0 %collective-permute-start.2 = (f32[192,128]{1,0:T(8,128)S(1)}, f32[192,128]{1,0:T(8,128)S(1)}, u32[]{:S(2)}, u32[]{:S(2)}) collective-permute-start(f32[192,128]{1,0:T(8,128)S(1)} %get-tuple-element.26.refs_0_), channel_id=1, source_target_pairs={{0,6},{1,7},{2,4},{3,5},{4,2},{5,3},{6,0},{7,1},{8,14},{9,15},{10,... | collective-permute-start | bytes 294920 | tf_op jit(solution)/shard_map/ppermute | solution.py:452
  13.0 0.0 collective-permute-start.1
  13.0 0.0 collective-permute-done.5.refs_3_.refs_5_
  13.0 0.6 %collective-permute-start = (f32[192,128]{1,0:T(8,128)S(1)}, f32[192,128]{1,0:T(8,128)S(1)}, u32[]{:S(2)}, u32[]{:S(2)}) collective-permute-start(f32[192,128]{1,0:T(8,128)S(1)} %get-tuple-element.26.refs_0_), channel_id=1, source_target_pairs={{0,2},{1,3},{2,0},{3,1},{4,6},{5,7},{6,4},{7,5},{8,10},{9,11},{10,... | collective-permute-start | bytes 294920 | tf_op jit(solution)/shard_map/ppermute | solution.py:452
  14.2 0.0 collective-permute-done.4.refs_2_.refs_4_
  14.2 3.3 %shard_map.77 = (f32[3,256,2048]{2,1,0:T(8,128)S(1)}, bf16[256,2048]{1,0:T(8,128)(2,1)S(1)}, bf16[192,2048]{1,0:T(8,128)(2,1)S(1)}, bf16[2048,64]{1,0:T(8,128)(2...) custom-call(f32[64,384]{1,0:T(8,128)S(1)} %get-tuple-element.27.refs, ...), custom_call_target="tpu_custom_call" | custom-call | tf_op jit(solution)/shard_map/pallas_call | solution.py:392
  17.6 2.8 %collective-permute-done.1.refs_2_ = f32[192,128]{1,0:T(8,128)S(1)} collective-permute-done((f32[192,128]{1,0:T(8,128)S(1)}, f32[192,128]{1,0:T(8,128)S(1)}, u32[]{:S(2)}, u32[]{:S(2)}) %collective-permute-start.1) | collective-permute-done | bytes 98336 | tf_op jit(solution)/shard_map/ppermute | solution.py:452
  20.4 0.0 collective-permute-done.refs_1_
  20.4 15.6 %shard_map.78 = (f32[256,192]{1,0:T(8,128)S(1)}, f32[512,192]{1,0:T(8,128)S(1)}, f32[3,512,2048]{2,1,0:T(8,128)S(1)}, bf16[512,2048]{1,0:T(8,128)(2,1)S(1)}, bf1...) custom-call(f32[192,128]{1,0:T(8,128)S(1)} %get-tuple-element.26.refs_0_, ...), custom_call_target="tpu_custom_call" | custom-call | tf_op jit(solution)/shard_map/pallas_call | solution.py:392
  36.0 0.1 collective-permute-start.6
  36.1 1.5 %collective-permute-done.6.refs_1_ = f32[256,192]{1,0:T(8,128)S(1)} collective-permute-done((f32[256,192]{1,0:T(8,128)S(1)}, f32[256,192]{1,0:T(8,128)S(1)}, u32[]{:S(2)}, u32[]{:S(2)}) %collective-permute-start.6) | collective-permute-done | bytes 196640 | tf_op jit(solution)/shard_map/ppermute | solution.py:485
  37.6 11.9 %shard_map.79 = (f32[256,192]{1,0:T(8,128)S(1)}, f32[512,192]{1,0:T(8,128)S(1)}, f32[512,192]{1,0:T(8,128)S(1)}) custom-call(f32[256,192]{1,0:T(8,128)S(1)} %get-tuple-element.37.refs_0_, f32[256,192]{1,0:T(8,128)S(1)} %collective-permute-done.6.refs_1_, f32[64,384]{1,0:T(8,128)S(1)} %get-tuple-element.27.refs_0_.refs_2_, ...), custom_call_target="tpu_custom_call" | custom-call | tf_op jit(solution)/shard_map/pallas_call | solution.py:392
  49.5 0.2 collective-permute-start.7
  49.7 1.7 %shard_map.80 = (f32[192,128]{1,0:T(8,128)}, f32[2016,128]{1,0:T(8,128)}) custom-call(f32[512,192]{1,0:T(8,128)S(1)} %get-tuple-element.44.coeffs, bf16[192,2048]{1,0:T(8,128)(2,1)S(1)} %get-tuple-element.31.refs_7_.refs_9_.inc.refs_5_, f32[3,512,2048]{2,1,0:T(8,128)S(1)} %get-tuple-element.39.refs_11_.grad_i.refs_7_), custom_call_target="tpu_custom_call" | custom-call | tf_op jit(solution)/shard_map/pallas_call | solution.py:392
  51.4 0.0 collective-permute-done.7.refs_1_
  51.4 4.2 %shard_map.81 = f32[192,128]{1,0:T(8,128)} custom-call(f32[256,192]{1,0:T(8,128)S(1)} %get-tuple-element.46.refs_0_, f32[256,192]{1,0:T(8,128)S(1)} %collective-permute-done.7.refs_1_, f32[512,192]{1,0:T(8,128)S(1)} %get-tuple-element.47.refs_2_, f32[3,256,2048]{2,1,0:T(8,128)S(1)} %get-tuple-element.29.refs_5_.refs_7_.refs_3_, ...), custom_call_target="tpu_custom_call" | custom-call | tf_op jit(solution)/shard_map/pallas_call | solution.py:392
  (6 shorter events, 0.0 us)
Async XLA Ops:
  0.6 0.9 %copy-start = (f32[128,192]{0,1:T(8,128)S(1)}, f32[128,192]{0,1:T(8,128)}, u32[]{:S(2)}) copy-start(f32[128,192]{0,1:T(8,128)} %param.6) | copy-start | bytes 294916
  1.5 0.8 %copy-start.1 = (f32[64,192]{1,0:T(8,128)S(1)}, f32[64,192]{1,0:T(8,128)}, u32[]{:S(2)}) copy-start(f32[64,192]{1,0:T(8,128)} %coords.1) | copy-start | bytes 147460
  2.4 0.8 %copy-start.2 = (f32[64,192]{1,0:T(8,128)S(1)}, f32[64,192]{1,0:T(8,128)}, u32[]{:S(2)}) copy-start(f32[64,192]{1,0:T(8,128)} %forces.1) | copy-start | bytes 147460
  3.2 0.7 %copy-start.3 = (s32[2,2016]{1,0:T(2,128)S(1)}, s32[2,2016]{1,0:T(2,128)}, u32[]{:S(2)}) copy-start(s32[2,2016]{1,0:T(2,128)} %pairs.1) | copy-start | bytes 48388
  4.3 8.6 %collective-permute-start.5 = (f32[64,384]{1,0:T(8,128)S(1)}, f32[64,384]{1,0:T(8,128)S(1)}, u32[]{:S(2)}, u32[]{:S(2)}) collective-permute-start(f32[64,384]{1,0:T(8,128)S(1)} %get-tuple-element.27.refs_0_.refs_2_), channel_id=1, source_target_pairs={{0,24},{8,16},{16,8},{24,0},{1,25},{9,17},{17,9},{25,1},{2,26},{10... | collective-permute-start | bytes 294920 | tf_op jit(solution)/shard_map/ppermute | solution.py:404
  8.3 5.9 %collective-permute-start.4 = (f32[64,384]{1,0:T(8,128)S(1)}, f32[64,384]{1,0:T(8,128)S(1)}, u32[]{:S(2)}, u32[]{:S(2)}) collective-permute-start(f32[64,384]{1,0:T(8,128)S(1)} %get-tuple-element.27.refs_0_.refs_2_), channel_id=1, source_target_pairs={{0,16},{8,24},{16,0},{24,8},{1,17},{9,25},{17,1},{25,9},{2,18},{10... | collective-permute-start | bytes 294920 | tf_op jit(solution)/shard_map/ppermute | solution.py:404
  8.8 5.4 %collective-permute-start.3 = (f32[64,384]{1,0:T(8,128)S(1)}, f32[64,384]{1,0:T(8,128)S(1)}, u32[]{:S(2)}, u32[]{:S(2)}) collective-permute-start(f32[64,384]{1,0:T(8,128)S(1)} %get-tuple-element.27.refs_0_.refs_2_), channel_id=1, source_target_pairs={{0,8},{8,0},{16,24},{24,16},{1,9},{9,1},{17,25},{25,17},{2,10},{10... | collective-permute-start | bytes 294920 | tf_op jit(solution)/shard_map/ppermute | solution.py:404
  9.0 8.6 %collective-permute-start.2 = (f32[192,128]{1,0:T(8,128)S(1)}, f32[192,128]{1,0:T(8,128)S(1)}, u32[]{:S(2)}, u32[]{:S(2)}) collective-permute-start(f32[192,128]{1,0:T(8,128)S(1)} %get-tuple-element.26.refs_0_), channel_id=1, source_target_pairs={{0,6},{1,7},{2,4},{3,5},{4,2},{5,3},{6,0},{7,1},{8,14},{9,15},{10,... | collective-permute-start | bytes 294920 | tf_op jit(solution)/shard_map/ppermute | solution.py:452
  13.0 7.4 %collective-permute-start.1 = (f32[192,128]{1,0:T(8,128)S(1)}, f32[192,128]{1,0:T(8,128)S(1)}, u32[]{:S(2)}, u32[]{:S(2)}) collective-permute-start(f32[192,128]{1,0:T(8,128)S(1)} %get-tuple-element.26.refs_0_), channel_id=1, source_target_pairs={{0,4},{1,5},{2,6},{3,7},{4,0},{5,1},{6,2},{7,3},{8,12},{9,13},{10,... | collective-permute-start | bytes 294920 | tf_op jit(solution)/shard_map/ppermute | solution.py:452
  13.0 7.4 %collective-permute-start = (f32[192,128]{1,0:T(8,128)S(1)}, f32[192,128]{1,0:T(8,128)S(1)}, u32[]{:S(2)}, u32[]{:S(2)}) collective-permute-start(f32[192,128]{1,0:T(8,128)S(1)} %get-tuple-element.26.refs_0_), channel_id=1, source_target_pairs={{0,2},{1,3},{2,0},{3,1},{4,6},{5,7},{6,4},{7,5},{8,10},{9,11},{10,... | collective-permute-start | bytes 294920 | tf_op jit(solution)/shard_map/ppermute | solution.py:452
  36.0 1.6 %collective-permute-start.6 = (f32[256,192]{1,0:T(8,128)S(1)}, f32[256,192]{1,0:T(8,128)S(1)}, u32[]{:S(2)}, u32[]{:S(2)}) collective-permute-start(f32[256,192]{1,0:T(8,128)S(1)} %get-tuple-element.37.refs_0_), channel_id=1, source_target_pairs={{0,1},{1,0},{2,3},{3,2},{4,5},{5,4},{6,7},{7,6},{8,9},{9,8},{10,11... | collective-permute-start | bytes 589832 | tf_op jit(solution)/shard_map/ppermute | solution.py:485
  49.5 1.9 %collective-permute-start.7 = (f32[256,192]{1,0:T(8,128)S(1)}, f32[256,192]{1,0:T(8,128)S(1)}, u32[]{:S(2)}, u32[]{:S(2)}) collective-permute-start(f32[256,192]{1,0:T(8,128)S(1)} %get-tuple-element.46.refs_0_), channel_id=1, source_target_pairs={{0,1},{1,0},{2,3},{3,2},{4,5},{5,4},{6,7},{7,6},{8,9},{9,8},{10,11... | collective-permute-start | bytes 589832 | tf_op jit(solution)/shard_map/ppermute | solution.py:485

commit v4 on v3

--- a/solution.py
+++ b/solution.py
@@ -388,7 +388,7 @@
 def call(body, limit, ins, outs, scratch, fetch=False):
     vmem = pl.BlockSpec(memory_space=pltpu.VMEM)
     smem = pl.BlockSpec(memory_space=pltpu.SMEM)
-    hbm = pl.BlockSpec(memory_space=pl.ANY)
+    hbm = pl.BlockSpec(memory_space=pltpu.HBM)
     return pl.pallas_call(
         body,
         in_specs=[hbm if fetch else smem if x.ndim == 1 else vmem for x in ins],
@@ -439,10 +439,11 @@
     def pin(xs):
         return [pltpu.with_memory_space_constraint(x, pltpu.VMEM) for x in xs] if stays else xs
 
+    fetched = [train_coords, train_forces, induce_coords.T, atom_pairs]
     both, turned, pairs = call(
         join_kernel,
         limit,
-        [train_coords, train_forces, induce_coords.T, atom_pairs],
+        [pltpu.with_memory_space_constraint(x, pltpu.HBM) for x in fetched],
         [kept((train_coords.shape[0], 6 * atoms), f32), kept((3 * atoms, own), f32), kept(atom_pairs.shape, atom_pairs.dtype)],
         [pltpu.VMEM(train_coords.shape, f32)] * 2 + [pltpu.SemaphoreType.DMA((4,))],
         fetch=True,

time: 56 us -> 53.5 us (0.955)
  local copies, waits for them, and re-layouts: 3.28 us -> 0 us
  Pallas kernels: 37.2 us -> 38.1 us
    unnamed x8 -> x0, local copies, waits for them, and re-layouts: 3.28 us -> none
    pallas_call x6, Pallas kernels: 37.2 us -> 38.1 us  [call(): pl.pallas_call(body, in_specs=[hbm if fetch else smem if x.ndim == 1 else...]
where the time goes in v4:
time: 53.5 us; the launch traced here: 53.3 us
  Pallas kernels  38.1 us (71%)
  starting transfers between devices  9.47 us (18%)
  waiting for transfers between devices  4.37 us (8%)
  between operations  1.34 us (3%)
    pallas_call x6, Pallas kernels, call(): pl.pallas_call(body, in_specs=[hbm if fetch else smem if x.ndim == 1 else...  38.1 us
    ppermute x3, starting transfers between devices, gather_rows(): lax.ppermute(x, axis, [(i, i ^ step) for i in range(size)])  4.63 us
    ppermute x3, starting transfers between devices, per_device(): lax.ppermute(turned, 'induce', [(i, i ^ 2 * step) for i in range(n_induce)])  4.57 us
    ppermute x3, waiting for transfers between devices, per_device(): lax.ppermute(turned, 'induce', [(i, i ^ 2 * step) for i in range(n_induce)])  2.84 us
    ppermute x2, waiting for transfers between devices, reduce_parts(): lax.ppermute(x, 'induce', [(i, i ^ 1) for i in range(n_induce)])  1.52 us
  transfers between devices with their start and end apart: 8, of which 2 were waited for; matrix products, arithmetic and copies ran while one was open for 0% of the time, Pallas kernels for 9%

profile of v4, /device:TPU:0, one launch (start us, length us, event | category | flops | bytes accessed | tf_op | source)
XLA Modules:
  0.0 53.3 jit_solution(15751654280427020559)
XLA Ops:
  0.6 1.1 %shard_map.76 = (f32[64,384]{1,0:T(8,128)S(1)}, f32[192,128]{1,0:T(8,128)S(1)}, s32[2,2016]{1,0:T(2,128)S(1)}) custom-call(f32[64,192]{1,0:T(8,128)} %coords.1, f32[64,192]{1,0:T(8,128)} %forces.1, f32[192,128]{1,0:T(8,128)} %bitcast.5, s32[2,2016]{1,0:T(2,128)} %pairs.1), custom_call_target="tpu_custom_call" | custom-call | tf_op jit(solution)/shard_map/pallas_call | solution.py:392
  1.7 4.0 %collective-permute-start.5 = (f32[64,384]{1,0:T(8,128)S(1)}, f32[64,384]{1,0:T(8,128)S(1)}, u32[]{:S(2)}, u32[]{:S(2)}) collective-permute-start(f32[64,384]{1,0:T(8,128)S(1)} %get-tuple-element.27.refs_0_.refs_2_), channel_id=1, source_target_pairs={{0,24},{8,16},{16,8},{24,0},{1,25},{9,17},{17,9},{25,1},{2,26},{10... | collective-permute-start | bytes 294920 | tf_op jit(solution)/shard_map/ppermute | solution.py:404
  5.7 0.5 collective-permute-start.4
  6.2 0.1 collective-permute-start.3
  6.4 4.0 %collective-permute-start.2 = (f32[192,128]{1,0:T(8,128)S(1)}, f32[192,128]{1,0:T(8,128)S(1)}, u32[]{:S(2)}, u32[]{:S(2)}) collective-permute-start(f32[192,128]{1,0:T(8,128)S(1)} %get-tuple-element.26.refs_0_), channel_id=1, source_target_pairs={{0,6},{1,7},{2,4},{3,5},{4,2},{5,3},{6,0},{7,1},{8,14},{9,15},{10,... | collective-permute-start | bytes 294920 | tf_op jit(solution)/shard_map/ppermute | solution.py:453
  10.4 0.0 collective-permute-start.1
  10.4 0.0 collective-permute-done.5.refs_3_.refs_5_
  10.4 0.6 %collective-permute-start = (f32[192,128]{1,0:T(8,128)S(1)}, f32[192,128]{1,0:T(8,128)S(1)}, u32[]{:S(2)}, u32[]{:S(2)}) collective-permute-start(f32[192,128]{1,0:T(8,128)S(1)} %get-tuple-element.26.refs_0_), channel_id=1, source_target_pairs={{0,2},{1,3},{2,0},{3,1},{4,6},{5,7},{6,4},{7,5},{8,10},{9,11},{10,... | collective-permute-start | bytes 294920 | tf_op jit(solution)/shard_map/ppermute | solution.py:453
  11.6 0.0 collective-permute-done.4.refs_2_.refs_4_
  11.6 0.0 collective-permute-done.3.refs_1_.refs_3_
  11.6 3.3 %shard_map.77 = (f32[3,256,2048]{2,1,0:T(8,128)S(1)}, bf16[256,2048]{1,0:T(8,128)(2,1)S(1)}, bf16[192,2048]{1,0:T(8,128)(2,1)S(1)}, bf16[2048,64]{1,0:T(8,128)(2...) custom-call(f32[64,384]{1,0:T(8,128)S(1)} %get-tuple-element.27.refs, ...), custom_call_target="tpu_custom_call" | custom-call | tf_op jit(solution)/shard_map/pallas_call | solution.py:392
  14.9 0.0 collective-permute-done.2.refs_3_
  14.9 2.8 %collective-permute-done.1.refs_2_ = f32[192,128]{1,0:T(8,128)S(1)} collective-permute-done((f32[192,128]{1,0:T(8,128)S(1)}, f32[192,128]{1,0:T(8,128)S(1)}, u32[]{:S(2)}, u32[]{:S(2)}) %collective-permute-start.1) | collective-permute-done | bytes 98336 | tf_op jit(solution)/shard_map/ppermute | solution.py:453
  17.8 0.0 collective-permute-done.refs_1_
  17.8 15.8 %shard_map.78 = (f32[256,192]{1,0:T(8,128)S(1)}, f32[512,192]{1,0:T(8,128)S(1)}, f32[3,512,2048]{2,1,0:T(8,128)S(1)}, bf16[512,2048]{1,0:T(8,128)(2,1)S(1)}, bf1...) custom-call(f32[192,128]{1,0:T(8,128)S(1)} %get-tuple-element.26.refs_0_, ...), custom_call_target="tpu_custom_call" | custom-call | tf_op jit(solution)/shard_map/pallas_call | solution.py:392
  33.6 0.1 collective-permute-start.6
  33.7 1.5 %collective-permute-done.6.refs_1_ = f32[256,192]{1,0:T(8,128)S(1)} collective-permute-done((f32[256,192]{1,0:T(8,128)S(1)}, f32[256,192]{1,0:T(8,128)S(1)}, u32[]{:S(2)}, u32[]{:S(2)}) %collective-permute-start.6) | collective-permute-done | bytes 196640 | tf_op jit(solution)/shard_map/ppermute | solution.py:486
  35.2 12.0 %shard_map.79 = (f32[256,192]{1,0:T(8,128)S(1)}, f32[512,192]{1,0:T(8,128)S(1)}, f32[512,192]{1,0:T(8,128)S(1)}) custom-call(f32[256,192]{1,0:T(8,128)S(1)} %get-tuple-element.37.refs_0_, f32[256,192]{1,0:T(8,128)S(1)} %collective-permute-done.6.refs_1_, f32[64,384]{1,0:T(8,128)S(1)} %get-tuple-element.27.refs_0_.refs_2_, ...), custom_call_target="tpu_custom_call" | custom-call | tf_op jit(solution)/shard_map/pallas_call | solution.py:392
  47.2 0.2 collective-permute-start.7
  47.4 1.7 %shard_map.80 = (f32[192,128]{1,0:T(8,128)}, f32[2016,128]{1,0:T(8,128)}) custom-call(f32[512,192]{1,0:T(8,128)S(1)} %get-tuple-element.44.coeffs, bf16[192,2048]{1,0:T(8,128)(2,1)S(1)} %get-tuple-element.31.refs_7_.refs_9_.inc.refs_5_, f32[3,512,2048]{2,1,0:T(8,128)S(1)} %get-tuple-element.39.refs_11_.grad_i.refs_7_), custom_call_target="tpu_custom_call" | custom-call | tf_op jit(solution)/shard_map/pallas_call | solution.py:392
  49.0 0.0 collective-permute-done.7.refs_1_
  49.1 4.2 %shard_map.81 = f32[192,128]{1,0:T(8,128)} custom-call(f32[256,192]{1,0:T(8,128)S(1)} %get-tuple-element.46.refs_0_, f32[256,192]{1,0:T(8,128)S(1)} %collective-permute-done.7.refs_1_, f32[512,192]{1,0:T(8,128)S(1)} %get-tuple-element.47.refs_2_, f32[3,256,2048]{2,1,0:T(8,128)S(1)} %get-tuple-element.29.refs_5_.refs_7_.refs_3_, ...), custom_call_target="tpu_custom_call" | custom-call | tf_op jit(solution)/shard_map/pallas_call | solution.py:392
Async XLA Ops:
  1.7 8.6 %collective-permute-start.5 = (f32[64,384]{1,0:T(8,128)S(1)}, f32[64,384]{1,0:T(8,128)S(1)}, u32[]{:S(2)}, u32[]{:S(2)}) collective-permute-start(f32[64,384]{1,0:T(8,128)S(1)} %get-tuple-element.27.refs_0_.refs_2_), channel_id=1, source_target_pairs={{0,24},{8,16},{16,8},{24,0},{1,25},{9,17},{17,9},{25,1},{2,26},{10... | collective-permute-start | bytes 294920 | tf_op jit(solution)/shard_map/ppermute | solution.py:404
  5.7 5.9 %collective-permute-start.4 = (f32[64,384]{1,0:T(8,128)S(1)}, f32[64,384]{1,0:T(8,128)S(1)}, u32[]{:S(2)}, u32[]{:S(2)}) collective-permute-start(f32[64,384]{1,0:T(8,128)S(1)} %get-tuple-element.27.refs_0_.refs_2_), channel_id=1, source_target_pairs={{0,16},{8,24},{16,0},{24,8},{1,17},{9,25},{17,1},{25,9},{2,18},{10... | collective-permute-start | bytes 294920 | tf_op jit(solution)/shard_map/ppermute | solution.py:404
  6.2 5.4 %collective-permute-start.3 = (f32[64,384]{1,0:T(8,128)S(1)}, f32[64,384]{1,0:T(8,128)S(1)}, u32[]{:S(2)}, u32[]{:S(2)}) collective-permute-start(f32[64,384]{1,0:T(8,128)S(1)} %get-tuple-element.27.refs_0_.refs_2_), channel_id=1, source_target_pairs={{0,8},{8,0},{16,24},{24,16},{1,9},{9,1},{17,25},{25,17},{2,10},{10... | collective-permute-start | bytes 294920 | tf_op jit(solution)/shard_map/ppermute | solution.py:404
  6.4 8.6 %collective-permute-start.2 = (f32[192,128]{1,0:T(8,128)S(1)}, f32[192,128]{1,0:T(8,128)S(1)}, u32[]{:S(2)}, u32[]{:S(2)}) collective-permute-start(f32[192,128]{1,0:T(8,128)S(1)} %get-tuple-element.26.refs_0_), channel_id=1, source_target_pairs={{0,6},{1,7},{2,4},{3,5},{4,2},{5,3},{6,0},{7,1},{8,14},{9,15},{10,... | collective-permute-start | bytes 294920 | tf_op jit(solution)/shard_map/ppermute | solution.py:453
  10.4 7.4 %collective-permute-start.1 = (f32[192,128]{1,0:T(8,128)S(1)}, f32[192,128]{1,0:T(8,128)S(1)}, u32[]{:S(2)}, u32[]{:S(2)}) collective-permute-start(f32[192,128]{1,0:T(8,128)S(1)} %get-tuple-element.26.refs_0_), channel_id=1, source_target_pairs={{0,4},{1,5},{2,6},{3,7},{4,0},{5,1},{6,2},{7,3},{8,12},{9,13},{10,... | collective-permute-start | bytes 294920 | tf_op jit(solution)/shard_map/ppermute | solution.py:453
  10.4 7.4 %collective-permute-start = (f32[192,128]{1,0:T(8,128)S(1)}, f32[192,128]{1,0:T(8,128)S(1)}, u32[]{:S(2)}, u32[]{:S(2)}) collective-permute-start(f32[192,128]{1,0:T(8,128)S(1)} %get-tuple-element.26.refs_0_), channel_id=1, source_target_pairs={{0,2},{1,3},{2,0},{3,1},{4,6},{5,7},{6,4},{7,5},{8,10},{9,11},{10,... | collective-permute-start | bytes 294920 | tf_op jit(solution)/shard_map/ppermute | solution.py:453
  33.6 1.6 %collective-permute-start.6 = (f32[256,192]{1,0:T(8,128)S(1)}, f32[256,192]{1,0:T(8,128)S(1)}, u32[]{:S(2)}, u32[]{:S(2)}) collective-permute-start(f32[256,192]{1,0:T(8,128)S(1)} %get-tuple-element.37.refs_0_), channel_id=1, source_target_pairs={{0,1},{1,0},{2,3},{3,2},{4,5},{5,4},{6,7},{7,6},{8,9},{9,8},{10,11... | collective-permute-start | bytes 589832 | tf_op jit(solution)/shard_map/ppermute | solution.py:486
  47.2 1.9 %collective-permute-start.7 = (f32[256,192]{1,0:T(8,128)S(1)}, f32[256,192]{1,0:T(8,128)S(1)}, u32[]{:S(2)}, u32[]{:S(2)}) collective-permute-start(f32[256,192]{1,0:T(8,128)S(1)} %get-tuple-element.46.refs_0_), channel_id=1, source_target_pairs={{0,1},{1,0},{2,3},{3,2},{4,5},{5,4},{6,7},{7,6},{8,9},{9,8},{10,11... | collective-permute-start | bytes 589832 | tf_op jit(solution)/shard_map/ppermute | solution.py:486
